TPU v7x, 32 devices: a whole 2x2x4 slice. The times are simulated.
32 devices in a mesh: tok: 4 (over y, core), cache: 8 (over z, x).
Axes of the slice: x: 2, y: 2, z: 4, core: 2. Of those that a mesh axis runs over, the one named last changes fastest.
Arguments:
- queries_one: bfloat16 [64, 6, 128, 576], P('cache', None, 'tok'), may hold values from -100 to 100
- keys_one: bfloat16 [64, 6, 576], P('cache'), may hold values from -12 to 12
- queries_two: bfloat16 [64, 6, 128, 576], P('cache', None, 'tok'), may hold values from -100 to 100
- keys_two: bfloat16 [64, 6, 576], P('cache'), may hold values from -12 to 12
- latent_cache: bfloat16 [64, 640, 576], P('cache'), may hold values from -8 to 8
- cached_len: int32 [64], P('cache'), may hold values from 80 to 640
- first_owner: int32 [64], P('cache'), may hold values from 0 to 7, as said below
- new_owner: int32 [64], P('cache'), may hold values from 0 to 7, as said below
- accepted: int32 [64], P('cache'), may hold values from 1 to 6
Outputs:
- first_out: bfloat16 [64, 6, 128, 512], P('cache', None, 'tok')
- second_out: bfloat16 [64, 6, 128, 512], P('cache', None, 'tok')
- arrived_cache: bfloat16 [32, 640, 576], P('cache')
Inputs may be any that keep to these rules, and one draw needn't show every extreme that they name: `first_owner`: row j of a device's 8 draft rows is the request whose cache lies in slot j of the named cache device in round one; the rows of one device name every cache device exactly once, and every slot is named by exactly one row. `new_owner`: each slot's cache keeps its position j in round two. On every device the same half of the positions j name another device and the rest the device itself; the other devices that one device names are distinct, and every device receives exactly one cache into each slot that it gives up. The round-two devices of one device's draft rows name no cache device more than 2 times, and on every device some cache device exactly 2 times.
All inputs are finite; a program needn't handle non-finite values.
Results may differ from a plain program's by a relative error of at most 0.0032.
Values may be sent and summed in bfloat16 or wider, within the bound.
No kernel may reach another device: no remote copies, remote signals or barrier semaphores. Data moves between devices by JAX's collectives and lax.ppermute only.
A program may use at most 128 MiB of HBM per device.

v0:
```python
import functools

import jax
import jax.numpy as jnp
from jax import lax
from jax.experimental import pallas as pl
from jax.experimental.pallas import tpu as pltpu
from jax.sharding import PartitionSpec as P


LAT = 512
CORES = 2
ROWS = 16
LATE = 2

score_factor = 192.0 ** (-0.5)
log2_e = 1.4426950408889634
FREE = pl.BlockSpec(memory_space=pl.ANY)
ANY = pl.BlockSpec(memory_space=pl.ANY)
SMEM = pl.BlockSpec(memory_space=pltpu.SMEM)
VMEM = pl.BlockSpec(memory_space=pltpu.VMEM)


def round_up(value, step):
    return -(-value // step) * step


def tell_kernel(first_ref, length_ref, move_ref, out_ref):
    reqs = first_ref.shape[0]
    lane = lax.broadcasted_iota(jnp.int32, out_ref.shape, 1)
    row = jnp.zeros(out_ref.shape, jnp.int32)
    for t, ref in enumerate((first_ref, length_ref, move_ref)):
        for j in range(reqs):
            row = jnp.where(lane == t * reqs + j, ref[j], row)
    out_ref[...] = row


def tell(first_owner, cached_len, new_owner, peers):
    return pl.pallas_call(
        tell_kernel,
        out_shape=jax.ShapeDtypeStruct((peers, 3 * first_owner.shape[0]), jnp.int32),
        in_specs=[SMEM] * 3,
        out_specs=VMEM,
        name="tell",
    )(first_owner, cached_len, new_owner)


def peer_of(me, half, s, to):
    side, place = me // half, me % half
    if s < half:
        return side * half + s
    shift = s - half if to else 2 * half - s
    return (1 - side) * half + lax.rem(place + shift, half)


def take_kernel(plan, half, moves, meta_ref, slots_ref, table_ref, *refs):
    outs, sems = refs[: len(plan)], refs[-1]
    me = meta_ref[0]
    for p, rows_ref in enumerate(refs[len(plan) : -1]):
        for i in range(half):
            peer = peer_of(me, half, p * half + i, False)
            row = jnp.int32(0)
            for j in range(2 * half):
                row = jnp.where(slots_ref[me, j] == peer, j, row)
            rows_ref[i] = row
    copies = []
    for out_ref, (first, part) in zip(outs, plan):
        base = pl.multiple_of(meta_ref[part], ROWS)
        for d in range(out_ref.shape[0]):
            peer = peer_of(me, half, first + d, True)
            slot = jnp.int32(0)
            for j in range(2 * half):
                if moves:
                    hit = (slots_ref[j] == peer) & (peer != me)
                else:
                    hit = slots_ref[peer, j] == me
                slot = jnp.where(hit, j, slot)
            copies.append(
                pltpu.make_async_copy(
                    table_ref.at[slot, pl.ds(base, out_ref.shape[1])],
                    out_ref.at[d],
                    sems.at[first + d],
                )
            )
    for copy in copies:
        copy.start()
    for copy in copies:
        copy.wait()


def take_rows(table, meta, slots, moves, plan, shapes):
    lanes = table.shape[2]
    count = sum(shape[0] for shape in shapes)
    lists = 0 if moves else 2
    size = sum(n * rows for n, rows in shapes) * lanes * table.dtype.itemsize
    return pl.pallas_call(
        functools.partial(take_kernel, plan, count // 2, moves),
        out_shape=[jax.ShapeDtypeStruct(shape + (lanes,), table.dtype) for shape in shapes]
        + [jax.ShapeDtypeStruct((count // 2,), jnp.int32)] * lists,
        in_specs=[SMEM, SMEM, ANY],
        out_specs=[VMEM] * len(shapes) + [SMEM] * lists,
        scratch_shapes=[pltpu.SemaphoreType.DMA((count,))],
        cost_estimate=pl.CostEstimate(flops=2 * size, bytes_accessed=2 * size, transcendentals=0),
        name="take_rows",
    )(meta, slots, table)


def place_kernel(groups, kept, half, meta_ref, heard_ref, move_ref, *refs):
    count = len(groups)
    reqs = move_ref.shape[0]
    me = meta_ref[0]
    order, leaves = [], []
    rank = jnp.int32(0)
    for j in range(reqs):
        leaves.append(move_ref[j] != me)
        order.append(rank)
        rank = rank + leaves[-1].astype(jnp.int32)
    dests = {}
    for source in sorted({source + i for source, i in spans_of(groups, refs)}):
        peer = peer_of(me, half, source, False)
        dest = jnp.int32(-1)
        for j in range(reqs):
            hit = leaves[j] & (heard_ref[peer, 2 * reqs + j] == me)
            dest = jnp.where(hit, order[j], dest)
        dests[source] = dest
    parts, out_ref, bufs = refs[:count], refs[count + kept], refs[count + kept + 1 : -2]
    in_sems, out_sems = refs[-2:]
    steps = []
    for p, (source, origin) in enumerate(groups):
        base = pl.multiple_of(meta_ref[origin], ROWS)
        for i in range(parts[p].shape[0]):
            dest = dests[source + i]
            load = pltpu.make_async_copy(parts[p].at[i], bufs[p].at[i], in_sems.at[p, i])
            store = pltpu.make_async_copy(
                bufs[p].at[i],
                out_ref.at[jnp.maximum(dest, 0), pl.ds(base, parts[p].shape[1])],
                out_sems.at[p, i],
            )
            steps.append((dest >= 0, load, store))
    for used, load, store in steps:
        pl.when(used)(load.start)
    for used, load, store in steps:

        @pl.when(used)
        def _(load=load, store=store):
            load.wait()
            store.start()

    for used, load, store in steps:
        pl.when(used)(store.wait)


def spans_of(groups, parts):
    return [(source, i) for (source, _), part in zip(groups, parts) for i in range(part.shape[0])]


def place_parts(parts, groups, meta, heard, moves, shape, out=None):
    dtype = parts[0].dtype
    size = shape[0] * shape[1] * shape[2] * dtype.itemsize
    kept = [] if out is None else [out]
    most = max(part.shape[0] for part in parts)
    return pl.pallas_call(
        functools.partial(place_kernel, groups, len(kept), heard.shape[0] // 2),
        out_shape=jax.ShapeDtypeStruct(shape, dtype),
        in_specs=[SMEM] * 3 + [FREE] * (len(parts) + len(kept)),
        out_specs=ANY,
        input_output_aliases={3 + len(parts): 0} if kept else {},
        scratch_shapes=[pltpu.VMEM(part.shape, dtype) for part in parts]
        + [pltpu.SemaphoreType.DMA((len(parts), most))] * 2,
        cost_estimate=pl.CostEstimate(flops=size, bytes_accessed=size, transcendentals=0),
        name="place_parts",
    )(meta, heard, moves, *parts, *kept)


def attend(queries, keys_t, length, extra, extra_mask):
    scale = score_factor * log2_e
    near = jnp.dot(queries, keys_t, preferred_element_type=jnp.float32) * scale
    places = lax.broadcasted_iota(jnp.int32, (1, keys_t.shape[1]), 1)
    near = jnp.where(places < length, near, -jnp.inf)
    own = (
        lax.dot_general(
            queries, extra, (((1,), (1,)), ((), ())), preferred_element_type=jnp.float32
        )
        * scale
    )
    own = jnp.where(extra_mask, own, -jnp.inf)
    row_max = jnp.maximum(
        jnp.max(near, axis=1, keepdims=True), jnp.max(own, axis=1, keepdims=True)
    )
    near_weight = jnp.exp2(near - row_max)
    own_weight = jnp.exp2(own - row_max)
    total = jnp.sum(near_weight, axis=1, keepdims=True) + jnp.sum(
        own_weight, axis=1, keepdims=True
    )
    mixture = lax.dot_general(
        near_weight.astype(jnp.bfloat16),
        keys_t[:LAT],
        (((1,), (1,)), ((), ())),
        preferred_element_type=jnp.float32,
    )
    mixture = mixture + jnp.dot(
        own_weight.astype(jnp.bfloat16), extra[:, :LAT], preferred_element_type=jnp.float32
    )
    return (mixture * (1.0 / total)).astype(jnp.bfloat16)


def attend_kernel(groups, kept, meta_ref, heard_ref, first_ref, accept_ref, row_ref, *refs):
    parts = refs[: len(groups)]
    q1_hbm, q2_hbm, k1_ref, k2_ref = refs[len(groups) : len(groups) + 4]
    o1_ref, o2_ref, held, q1_held, q2_held, sems, q_sems = refs[len(groups) + 4 + kept :]
    step = pl.program_id(0)
    base_slot = groups[0][0]

    def query_copies(index):
        for k, (src, dst) in enumerate(((q1_hbm, q1_held), (q2_hbm, q2_held))):
            yield pltpu.make_async_copy(src.at[row_ref[index]], dst.at[index], q_sems.at[index, k])

    @pl.when(step == 0)
    def _():
        used = {}
        loads = []
        for (request, origin), part in zip(groups, parts):
            base = pl.multiple_of(meta_ref[origin], ROWS)
            for i in range(part.shape[0]):
                slot = request + i - base_slot
                sem = used[slot] = used.get(slot, -1) + 1
                copy = pltpu.make_async_copy(
                    part.at[i], held.at[slot, pl.ds(base, part.shape[1])], sems.at[slot, sem]
                )
                loads.append((slot, copy))
        loads.sort(key=lambda load: load[0])
        for index in range(held.shape[0]):
            for copy in query_copies(index):
                copy.start()
            for slot, copy in loads:
                if slot == index:
                    copy.start()

    for copy in query_copies(step):
        copy.wait()
    request = row_ref[step]
    peer = first_ref[request]
    for p in range(sems.shape[1]):
        rows = parts[0].shape[1]
        pltpu.make_async_copy(
            parts[0].at[0], held.at[step, pl.ds(0, rows)], sems.at[step, p]
        ).wait()

    rows = q1_held.shape[1]
    reqs = first_ref.shape[0]
    draft = k1_ref.shape[0] // reqs
    heads = rows // draft
    keys = jnp.concatenate([k1_ref[...], k2_ref[...]], axis=0)
    row = lax.broadcasted_iota(jnp.int32, (2 * rows, 1), 0)
    col = lax.broadcasted_iota(jnp.int32, (1, keys.shape[0]), 1)
    key = lax.div(col, reqs)
    own = lax.rem(col, reqs) == request
    first = own & (key < draft)
    second = row >= rows
    causal = row - jnp.where(second, rows, 0) >= lax.rem(key, draft) * heads
    taken = first & (key < accept_ref[request])
    mask = (first & causal & ~second) | (
        (taken | (own & (key >= draft) & causal)) & second
    )
    keys_t = held[step]
    length = heard_ref[peer, reqs + request]
    queries = jnp.concatenate([q1_held[step], q2_held[step]], axis=0)
    out = attend(queries, keys_t, length, keys, mask)
    o1_ref[0] = out[:rows]
    o2_ref[0] = out[rows:]


def attend_some(q1, q2, k1, k2, parts, groups, meta, heard, first, accepted, rows_of, outs=()):
    reqs, rows, width = q1.shape
    count = rows_of.shape[0]
    positions = parts[0].shape[2]
    each = sum(part.shape[0] for part in parts) // count
    block = lambda lanes: pl.BlockSpec((1, rows, lanes), lambda r, *refs: (refs[4][r], 0, 0))
    whole = pl.BlockSpec(k1.shape, lambda r, *_: (0, 0))
    out = jax.ShapeDtypeStruct((reqs, rows, LAT), jnp.bfloat16)
    flops = 2 * 2 * count * rows * positions * (width + LAT)
    start = 5 + len(parts) + 4
    return pl.pallas_call(
        functools.partial(attend_kernel, groups, len(outs)),
        grid_spec=pltpu.PrefetchScalarGridSpec(
            num_scalar_prefetch=5,
            grid=(count,),
            in_specs=[ANY] * len(parts)
            + [ANY, ANY, whole, whole]
            + [ANY] * len(outs),
            out_specs=[block(LAT), block(LAT)],
            scratch_shapes=[
                pltpu.VMEM((count, width, positions), jnp.bfloat16),
                pltpu.VMEM((count, rows, width), jnp.bfloat16),
                pltpu.VMEM((count, rows, width), jnp.bfloat16),
                pltpu.SemaphoreType.DMA((count, each)),
                pltpu.SemaphoreType.DMA((count, 2)),
            ],
        ),
        out_shape=(out, out),
        input_output_aliases={start + i: i for i in range(len(outs))},
        cost_estimate=pl.CostEstimate(
            flops=flops, bytes_accessed=count * width * positions * 4, transcendentals=0
        ),
        compiler_params=pltpu.CompilerParams(dimension_semantics=("arbitrary",)),
        name="attend_some",
    )(meta, heard, first, accepted, rows_of, *parts, q1, q2, k1, k2, *outs)


def program(
    queries_one,
    keys_one,
    queries_two,
    keys_two,
    latent_cache,
    cached_len,
    first_owner,
    new_owner,
    accepted,
):
    peers = lax.axis_size("cache")
    me = lax.axis_index("cache")
    groups = lax.axis_size("tok")
    group = lax.axis_index("tok")
    chips = groups // CORES
    reqs, draft, heads, width = queries_one.shape
    half = peers // 2
    halves = [[h * half + i for i in range(half)] for h in range(2)]

    def near_exchange(x):
        return lax.all_to_all(
            x, "cache", split_axis=0, concat_axis=0, tiled=True, axis_index_groups=halves
        )

    def far_shift(x, s):
        hop = [
            (h * half + i, (1 - h) * half + (i + s) % half) for h in range(2) for i in range(half)
        ]
        return lax.ppermute(x, "cache", hop)

    told = tell(first_owner, cached_len, new_owner, peers)
    heard = lax.all_to_all(told, "cache", split_axis=0, concat_axis=0, tiled=True)

    cache_t = jnp.swapaxes(latent_cache, 1, 2)
    share = round_up(-(-width // groups), ROWS)
    start_of = lambda t: jnp.minimum(t * share, width - share).astype(jnp.int32)
    chip, core = group // CORES, group % CORES
    origins = [group] + [(chip + chips - s) % chips * CORES + core for s in range(1, chips)]
    origins += [t + 1 - 2 * core for t in origins]
    wide = round_up(-(-width // CORES), ROWS)
    wide_of = lambda k: jnp.minimum(k * wide, width - wide).astype(jnp.int32)
    meta = jnp.stack(
        [me.astype(jnp.int32)]
        + [start_of(t) for t in origins]
        + [wide_of(core), wide_of(1 - core)]
    )
    swap = [(t, t + 1 - 2 * (t % CORES)) for t in range(groups)]

    def spread(part):
        held = [part]
        for s in range(1, chips):
            hop = [
                (c * CORES + k, (c + s) % chips * CORES + k)
                for c in range(chips)
                for k in range(CORES)
            ]
            held.append(lax.ppermute(part, "tok", hop))
        for x in held[:]:
            held.append(lax.ppermute(x, "tok", swap))
        return held

    plan = [(0, groups + 1)] + [(half + s, 1) for s in range(half)]
    sent = take_rows(
        cache_t, meta, new_owner, True, plan, [(half, wide)] + [(1, share)] * half
    )
    move_far = []
    for s in range(half):
        move_far.append(far_shift(sent[1 + s], s))
    move_near = near_exchange(sent[0])

    plan = [(0, 1)] + [(half + s, 1) for s in range(half)]
    *sent, rows_near, rows_far = take_rows(
        cache_t, meta, heard, False, plan, [(half, share)] + [(1, share)] * half
    )
    draft_far = []
    for s in range(half):
        draft_far.append(far_shift(sent[1 + s], s))
    draft_near = near_exchange(sent[0])

    flat = (reqs, draft * heads, width)
    keys = (draft * reqs, width)
    operands = (
        queries_one.reshape(flat),
        queries_two.reshape(flat),
        jnp.swapaxes(keys_one, 0, 1).reshape(keys),
        jnp.swapaxes(keys_two, 0, 1).reshape(keys),
    )
    scalars = (meta, heard, first_owner, accepted)

    parts = spread(draft_near)
    where = [(0, 1 + k) for k in range(groups)]
    outs = attend_some(*operands, parts, where, *scalars, rows_near)
    parts, where = [], []
    for s in range(half):
        parts += spread(draft_far[s])
        where += [(half + s, 1 + k) for k in range(groups)]
    outs = attend_some(*operands, parts, where, *scalars, rows_far, outs)

    tables = (meta, heard, new_owner)
    shape = (peers // 2, width, cache_t.shape[2])
    parts = [move_near, lax.ppermute(move_near, "tok", swap)]
    where = [(0, groups + 1), (0, groups + 2)]
    early = half - LATE
    for s in range(half):
        if s == early:
            arrived = place_parts(parts, where, *tables, shape)
            parts, where = [], []
        parts += spread(move_far[s])
        where += [(half + s, 1 + k) for k in range(groups)]
    arrived = place_parts(parts, where, *tables, shape, arrived)

    shape = (reqs, draft, heads, LAT)
    return outs[0].reshape(shape), outs[1].reshape(shape), jnp.swapaxes(arrived, 1, 2)


def solution(mesh):
    placed = (
        P("cache", None, "tok", None),
        P("cache", None, None),
        P("cache", None, "tok", None),
        P("cache", None, None),
        P("cache", None, None),
        P("cache"),
        P("cache"),
        P("cache"),
        P("cache"),
    )
    return jax.shard_map(
        program,
        mesh=mesh,
        in_specs=placed,
        out_specs=(
            P("cache", None, "tok", None),
            P("cache", None, "tok", None),
            P("cache", None, None),
        ),
        check_vma=False,
    )
```

profile of v0, /device:TPU:0, one launch (start us, length us, event | category | flops | bytes accessed | tf_op | source)
XLA Modules:
  0.0 166.5 jit_solution(5604892864240326890)
XLA Ops:
  0.6 1.3 tell.1
  1.9 7.3 %all-to-all-start = ((s32[8,1,24]{2,1,0:T(1,128)}), s32[8,1,24]{2,1,0:T(1,128)S(1)}, u32[]{:S(2)}, u32[]{:S(2)}) async-start(s32[8,1,24]{2,1,0:T(1,128)} %bitcast.41), calls=%async_computation | async-start | bytes 8192 | tf_op jit(solution)/shard_map/all_to_all | solution.py:342
  9.2 0.6 stack.31.meta_ref
  9.8 5.8 %all-to-all-done = s32[8,1,24]{2,1,0:T(1,128)S(1)} async-done(((s32[8,1,24]{2,1,0:T(1,128)}), s32[8,1,24]{2,1,0:T(1,128)S(1)}, u32[]{:S(2)}, u32[]{:S(2)}) %all-to-all-start) | async-done | bytes 800 | tf_op jit(solution)/shard_map/all_to_all | solution.py:342
  15.6 0.6 copy-done.17
  16.2 3.4 %take_rows.2 = (bf16[4,144,640]{2,1,0:T(8,128)(2,1)}, bf16[1,144,640]{2,1,0:T(8,128)(2,1)}, bf16[1,144,640]{2,1,0:T(8,128)(2,1)}, bf16[1,144,640]{2,1,0:T(8,128)...) custom-call(s32[7]{0:T(128)} %stack.31.meta_ref, s32[8,24]{1,0:T(8,128)} %bitcast.32, ...), custom_call_target="tpu_custom_call" | custom-call | flops 2949120 | bytes 2949120 | tf_op jit(solution)/shard_map/take_rows/pallas_call | solution.py:96
  19.6 4.2 %all-to-all-start.1 = ((bf16[4,144,640]{2,1,0:T(8,128)(2,1)}), bf16[4,144,640]{2,1,0:T(8,128)(2,1)}, u32[]{:S(2)}, u32[]{:S(2)}) async-start(bf16[4,144,640]{2,1,0:T(8,128)(2,1)} %get-tuple-element.25), calls=%async_computation.1 | async-start | bytes 1474560 | tf_op jit(solution)/shard_map/all_to_all | solution.py:331
  23.9 4.0 %take_rows.3 = (bf16[4,288,640]{2,1,0:T(8,128)(2,1)}, bf16[1,144,640]{2,1,0:T(8,128)(2,1)}, bf16[1,144,640]{2,1,0:T(8,128)(2,1)}, bf16[1,144,640]{2,1,0:T(8,128)(2,1)}, bf16[1,144,640]{2,1,0:T(8,128)(2,1)}) custom-call(s32[7]{0:T(128)} %stack.31.meta_ref, s32[8]{0:T(128)} %move_ref.5, bf16[8,576,640]{2,1,0:T(8,128)(2,1)} %bitcast.24), custom_call_target="tpu_custom_call" | custom-call | flops 4423680 | bytes 4423680 | tf_op jit(solution)/shard_map/take_rows/pallas_call | solution.py:96
  27.9 0.0 copy-start.23
  28.0 5.1 %all-to-all-done.1.refs_0_ = bf16[4,144,640]{2,1,0:T(8,128)(2,1)} async-done(((bf16[4,144,640]{2,1,0:T(8,128)(2,1)}), bf16[4,144,640]{2,1,0:T(8,128)(2,1)}, u32[]{:S(2)}, u32[]{:S(2)}) %all-to-all-start.1) | async-done | bytes 737312 | tf_op jit(solution)/shard_map/all_to_all | solution.py:331
  33.1 3.6 %all-to-all-start.2 = ((bf16[4,288,640]{2,1,0:T(8,128)(2,1)}), bf16[4,288,640]{2,1,0:T(8,128)(2,1)S(1)}, u32[]{:S(2)}, u32[]{:S(2)}) async-start(bf16[4,288,640]{2,1,0:T(8,128)(2,1)} %get-tuple-element.32), calls=%async_computation.2 | async-start | bytes 2949120 | tf_op jit(solution)/shard_map/all_to_all | solution.py:331
  36.6 2.0 %collective-permute-start.19 = (bf16[1,144,640]{2,1,0:T(8,128)(2,1)S(1)}, bf16[1,144,640]{2,1,0:T(8,128)(2,1)S(1)}, u32[]{:S(2)}, u32[]{:S(2)}) collective-permute-start(bf16[1,144,640]{2,1,0:T(8,128)(2,1)S(1)} %copy-done.27), channel_id=1, source_target_pairs={{0,6},{1,7},{2,4},{3,5},{4,2},{5,3},{6,0},{7,1},{8,14},{9,15},{10,... | collective-permute-start | bytes 552968 | tf_op jit(solution)/shard_map/ppermute | solution.py:339
  38.6 3.3 %collective-permute-start.23 = (bf16[1,144,640]{2,1,0:T(8,128)(2,1)S(1)}, bf16[1,144,640]{2,1,0:T(8,128)(2,1)S(1)}, u32[]{:S(2)}, u32[]{:S(2)}) collective-permute-start(bf16[1,144,640]{2,1,0:T(8,128)(2,1)S(1)} %copy-done.26), channel_id=1, source_target_pairs={{0,7},{1,4},{2,5},{3,6},{4,3},{5,0},{6,1},{7,2},{8,15},{9,12},{10,... | collective-permute-start | bytes 552968 | tf_op jit(solution)/shard_map/ppermute | solution.py:339
  41.9 2.0 %collective-permute-start.32 = (bf16[1,144,640]{2,1,0:T(8,128)(2,1)S(1)}, bf16[1,144,640]{2,1,0:T(8,128)(2,1)}, u32[]{:S(2)}, u32[]{:S(2)}) collective-permute-start(bf16[1,144,640]{2,1,0:T(8,128)(2,1)S(1)} %copy-done.24), channel_id=1, source_target_pairs={{0,5},{1,6},{2,7},{3,4},{4,1},{5,2},{6,3},{7,0},{8,13},{9,14},{10,... | collective-permute-start | bytes 552968 | tf_op jit(solution)/shard_map/ppermute | solution.py:339
  43.9 1.5 collective-permute-start
  45.4 16.4 %collective-permute-done.19.refs_0_ = bf16[1,144,640]{2,1,0:T(8,128)(2,1)S(1)} collective-permute-done((bf16[1,144,640]{2,1,0:T(8,128)(2,1)S(1)}, bf16[1,144,640]{2,1,0:T(8,128)(2,1)S(1)}, u32[]{:S(2)}, u32[]{:S(2)}) %collective-permute-start.19) | collective-permute-done | bytes 184352 | tf_op jit(solution)/shard_map/ppermute | solution.py:339
  61.8 1.5 collective-permute-start.16
  63.3 0.1 collective-permute-start.4
  63.4 2.6 %collective-permute-done.28.refs_2_ = bf16[1,144,640]{2,1,0:T(8,128)(2,1)S(1)} collective-permute-done((bf16[1,144,640]{2,1,0:T(8,128)(2,1)S(1)}, bf16[1,144,640]{2,1,0:T(8,128)(2,1)S(1)}, u32[]{:S(2)}, u32[]{:S(2)}) %collective-permute-start.28) | collective-permute-done | bytes 184352 | tf_op jit(solution)/shard_map/ppermute | solution.py:339
  66.1 3.1 %collective-permute-start.8 = (bf16[1,144,640]{2,1,0:T(8,128)(2,1)S(1)}, bf16[1,144,640]{2,1,0:T(8,128)(2,1)S(1)}, u32[]{:S(2)}, u32[]{:S(2)}) collective-permute-start(bf16[1,144,640]{2,1,0:T(8,128)(2,1)S(1)} %copy-done.21), channel_id=1, source_target_pairs={{0,6},{1,7},{2,4},{3,5},{4,2},{5,3},{6,0},{7,1},{8,14},{9,15},{10,... | collective-permute-start | bytes 552968 | tf_op jit(solution)/shard_map/ppermute | solution.py:339
  69.2 3.9 %collective-permute-done.32.refs_6_ = bf16[1,144,640]{2,1,0:T(8,128)(2,1)} collective-permute-done((bf16[1,144,640]{2,1,0:T(8,128)(2,1)S(1)}, bf16[1,144,640]{2,1,0:T(8,128)(2,1)}, u32[]{:S(2)}, u32[]{:S(2)}) %collective-permute-start.32) | collective-permute-done | bytes 184352 | tf_op jit(solution)/shard_map/ppermute | solution.py:339
  73.1 16.4 %collective-permute-start.12 = (bf16[1,144,640]{2,1,0:T(8,128)(2,1)S(1)}, bf16[1,144,640]{2,1,0:T(8,128)(2,1)S(1)}, u32[]{:S(2)}, u32[]{:S(2)}) collective-permute-start(bf16[1,144,640]{2,1,0:T(8,128)(2,1)S(1)} %copy-done.20), channel_id=1, source_target_pairs={{0,7},{1,4},{2,5},{3,6},{4,3},{5,0},{6,1},{7,2},{8,15},{9,12},{10,... | collective-permute-start | bytes 552968 | tf_op jit(solution)/shard_map/ppermute | solution.py:339
  89.4 1.7 %collective-permute-done.refs_0_ = bf16[1,144,640]{2,1,0:T(8,128)(2,1)} collective-permute-done((bf16[1,144,640]{2,1,0:T(8,128)(2,1)S(1)}, bf16[1,144,640]{2,1,0:T(8,128)(2,1)}, u32[]{:S(2)}, u32[]{:S(2)}) %collective-permute-start) | collective-permute-done | bytes 184352 | tf_op jit(solution)/shard_map/ppermute | solution.py:339
  91.1 1.5 collective-permute-start.20
  92.7 0.5 collective-permute-start.24
  93.2 0.0 collective-permute-done.8.refs_8_
  93.2 0.0 collective-permute-start.30
  93.2 9.8 %collective-permute-done.12.refs_12_ = bf16[1,144,640]{2,1,0:T(8,128)(2,1)S(1)} collective-permute-done((bf16[1,144,640]{2,1,0:T(8,128)(2,1)S(1)}, bf16[1,144,640]{2,1,0:T(8,128)(2,1)S(1)}, u32[]{:S(2)}, u32[]{:S(2)}) %collective-permute-start.12) | collective-permute-done | bytes 184352 | tf_op jit(solution)/shard_map/ppermute | solution.py:339
  103.0 1.5 collective-permute-start.29
  104.6 0.7 copy-done.5
  105.2 0.1 collective-permute-start.27
  105.3 0.6 collective-permute-start.33
  105.9 2.8 %collective-permute-done.29.refs_3_ = bf16[1,144,640]{2,1,0:T(8,128)(2,1)} collective-permute-done((bf16[1,144,640]{2,1,0:T(8,128)(2,1)S(1)}, bf16[1,144,640]{2,1,0:T(8,128)(2,1)}, u32[]{:S(2)}, u32[]{:S(2)}) %collective-permute-start.29) | collective-permute-done | bytes 184352 | tf_op jit(solution)/shard_map/ppermute | solution.py:367
  108.6 0.0 collective-permute-start.2
  108.6 2.5 %collective-permute-start.1 = (bf16[1,144,640]{2,1,0:T(8,128)(2,1)}, bf16[1,144,640]{2,1,0:T(8,128)(2,1)}, u32[]{:S(2)}, u32[]{:S(2)}) collective-permute-start(bf16[1,144,640]{2,1,0:T(8,128)(2,1)} %collective-permute-done.refs_0_), channel_id=1, source_target_pairs={{0,16},{8,24},{16,0},{24,8},{1,17},{9,25},{17,1},{25,9},{2,18},{10... | collective-permute-start | bytes 552968 | tf_op jit(solution)/shard_map/ppermute | solution.py:367
  111.1 1.5 collective-permute-done.33.refs_7_
  112.6 1.5 collective-permute-start.5
  114.1 2.8 %collective-permute-done.1.refs_1_ = bf16[1,144,640]{2,1,0:T(8,128)(2,1)} collective-permute-done((bf16[1,144,640]{2,1,0:T(8,128)(2,1)}, bf16[1,144,640]{2,1,0:T(8,128)(2,1)}, u32[]{:S(2)}, u32[]{:S(2)}) %collective-permute-start.1) | collective-permute-done | bytes 184352 | tf_op jit(solution)/shard_map/ppermute | solution.py:367
  116.9 0.5 collective-permute-start.18
  117.4 0.1 collective-permute-start.10
  117.5 3.2 %collective-permute-done.5.refs_5_ = bf16[1,144,640]{2,1,0:T(8,128)(2,1)} collective-permute-done((bf16[1,144,640]{2,1,0:T(8,128)(2,1)}, bf16[1,144,640]{2,1,0:T(8,128)(2,1)}, u32[]{:S(2)}, u32[]{:S(2)}) %collective-permute-start.5) | collective-permute-done | bytes 184352 | tf_op jit(solution)/shard_map/ppermute | solution.py:367
  120.7 1.7 %collective-permute-start.9 = (bf16[1,144,640]{2,1,0:T(8,128)(2,1)}, bf16[1,144,640]{2,1,0:T(8,128)(2,1)}, u32[]{:S(2)}, u32[]{:S(2)}) collective-permute-start(bf16[1,144,640]{2,1,0:T(8,128)(2,1)} %copy-done.11), channel_id=1, source_target_pairs={{0,16},{8,24},{16,0},{24,8},{1,17},{9,25},{17,1},{25,9},{2,18},{10... | collective-permute-start | bytes 552968 | tf_op jit(solution)/shard_map/ppermute | solution.py:367
  122.4 5.0 %collective-permute-done.9.refs_9_ = bf16[1,144,640]{2,1,0:T(8,128)(2,1)} collective-permute-done((bf16[1,144,640]{2,1,0:T(8,128)(2,1)}, bf16[1,144,640]{2,1,0:T(8,128)(2,1)}, u32[]{:S(2)}, u32[]{:S(2)}) %collective-permute-start.9) | collective-permute-done | bytes 184352 | tf_op jit(solution)/shard_map/ppermute | solution.py:367
  127.5 1.5 collective-permute-start.13
  128.9 0.1 collective-permute-start.31
  129.0 4.4 %collective-permute-done.13.refs_13_ = bf16[1,144,640]{2,1,0:T(8,128)(2,1)} collective-permute-done((bf16[1,144,640]{2,1,0:T(8,128)(2,1)}, bf16[1,144,640]{2,1,0:T(8,128)(2,1)}, u32[]{:S(2)}, u32[]{:S(2)}) %collective-permute-start.13) | collective-permute-done | bytes 184352 | tf_op jit(solution)/shard_map/ppermute | solution.py:367
  133.4 0.5 collective-permute-start.3
  133.9 0.9 collective-permute-done.35.refs_9_
  134.8 0.1 collective-permute-start.7
  135.0 0.5 copy-done.8
  135.5 0.2 collective-permute-start.11
  135.7 0.7 copy-done.18
  136.4 0.1 collective-permute-start.15
  136.5 0.7 copy-done.19
  137.3 9.9 %attend_some.2 = (bf16[8,192,512]{2,1,0:T(8,128)(2,1)}, bf16[8,192,512]{2,1,0:T(8,128)(2,1)}) custom-call(s32[7]{0:T(128)} %stack.31.meta_ref, s32[8,24]{1,0:T(8,128)} %bitcast.33, s32[8]{0:T(128)} %first_ref.5, s32[8]{0:T(128)} %accept_ref.3, s32[4]{0:T(128)} %get-tuple-element.24.row_ref, bf16[4,144,640]{2,1,0:T(8,128)(2,1)} %all-to-all-done.1.refs_0_, ...), custom_call_target="tpu_custom_call" | custom-call | flops 2139095040 | bytes 5898240 | tf_op jit(solution)/shard_map/attend_some/pallas_call | solution.py:283
  147.2 0.2 collective-permute-start.21
  147.4 0.4 collective-permute-start.25
  147.7 0.1 collective-permute-start.22
  147.9 0.4 collective-permute-start.26
  148.3 9.8 %attend_some.3 = (bf16[8,192,512]{2,1,0:T(8,128)(2,1)}, bf16[8,192,512]{2,1,0:T(8,128)(2,1)}) custom-call(s32[7]{0:T(128)} %stack.31.meta_ref, s32[8,24]{1,0:T(8,128)} %bitcast.34, s32[8]{0:T(128)} %first_ref.5, s32[8]{0:T(128)} %accept_ref.3, s32[4]{0:T(128)} %get-tuple-element.19.row_ref, ...), custom_call_target="tpu_custom_call", output_to_operand_aliasing={{0}: (25, {}), {1}: (26, {})} | custom-call | flops 2139095040 | bytes 5898240 | tf_op jit(solution)/shard_map/attend_some/pallas_call | solution.py:283
  158.1 1.1 copy-done.1
  159.2 3.6 %place_parts.2.refs_8_ = bf16[4,576,640]{2,1,0:T(8,128)(2,1)} custom-call(s32[7]{0:T(128)} %stack.31.meta_ref, s32[8,24]{1,0:T(8,128)} %bitcast.35, s32[8]{0:T(128)} %move_ref.5, bf16[4,288,640]{2,1,0:T(8,128)(2,1)} %copy-done, bf16[4,288,640]{2,1,0:T(8,128)(2,1)} %copy-done.1, bf16[1,144,640]{2,1,0:T(8,128)(2,1)} %copy-done.4, ...), custom_call_target="tpu_custom_call" | custom-call | flops 2949120 | bytes 2949120 | tf_op jit(solution)/shard_map/place_parts/pallas_call | solution.py:162
  162.8 0.6 copy-done.9
  163.5 3.0 %place_parts.3 = bf16[4,576,640]{2,1,0:T(8,128)(2,1)} custom-call(s32[7]{0:T(128)} %stack.31.meta_ref, s32[8,24]{1,0:T(8,128)} %bitcast.36, s32[8]{0:T(128)} %move_ref.5, bf16[1,144,640]{2,1,0:T(8,128)(2,1)} %copy-done.2, bf16[1,144,640]{2,1,0:T(8,128)(2,1)} %copy-done.5, bf16[1,144,640]{2,1,0:T(8,128)(2,1)} %copy-done.9, ...), custom_call_target="tpu_custom_call", output_to_operand_aliasing={{}: (11, {})} | custom-call | flops 2949120 | bytes 2949120 | tf_op jit(solution)/shard_map/place_parts/pallas_call | solution.py:162
  (78 shorter events, 0.2 us)
Async XLA Ops:
  1.9 13.7 %all-to-all-start = ((s32[8,1,24]{2,1,0:T(1,128)}), s32[8,1,24]{2,1,0:T(1,128)S(1)}, u32[]{:S(2)}, u32[]{:S(2)}) async-start(s32[8,1,24]{2,1,0:T(1,128)} %bitcast.41), calls=%async_computation | async-start | bytes 8192 | tf_op jit(solution)/shard_map/all_to_all | solution.py:342
  19.6 13.4 %all-to-all-start.1 = ((bf16[4,144,640]{2,1,0:T(8,128)(2,1)}), bf16[4,144,640]{2,1,0:T(8,128)(2,1)}, u32[]{:S(2)}, u32[]{:S(2)}) async-start(bf16[4,144,640]{2,1,0:T(8,128)(2,1)} %get-tuple-element.25), calls=%async_computation.1 | async-start | bytes 1474560 | tf_op jit(solution)/shard_map/all_to_all | solution.py:331
  27.9 8.8 %copy-start.27 = (bf16[1,144,640]{2,1,0:T(8,128)(2,1)S(1)}, bf16[1,144,640]{2,1,0:T(8,128)(2,1)}, u32[]{:S(2)}) copy-start(bf16[1,144,640]{2,1,0:T(8,128)(2,1)} %get-tuple-element.30) | copy-start | bytes 552964
  27.9 10.7 %copy-start.26 = (bf16[1,144,640]{2,1,0:T(8,128)(2,1)S(1)}, bf16[1,144,640]{2,1,0:T(8,128)(2,1)}, u32[]{:S(2)}) copy-start(bf16[1,144,640]{2,1,0:T(8,128)(2,1)} %get-tuple-element.31) | copy-start | bytes 552964
  27.9 14.0 %copy-start.25 = (bf16[1,144,640]{2,1,0:T(8,128)(2,1)S(1)}, bf16[1,144,640]{2,1,0:T(8,128)(2,1)}, u32[]{:S(2)}) copy-start(bf16[1,144,640]{2,1,0:T(8,128)(2,1)} %get-tuple-element.33) | copy-start | bytes 552964
  27.9 14.0 %copy-start.24 = (bf16[1,144,640]{2,1,0:T(8,128)(2,1)S(1)}, bf16[1,144,640]{2,1,0:T(8,128)(2,1)}, u32[]{:S(2)}) copy-start(bf16[1,144,640]{2,1,0:T(8,128)(2,1)} %get-tuple-element.34) | copy-start | bytes 552964
  27.9 16.0 %copy-start.23 = (bf16[1,144,640]{2,1,0:T(8,128)(2,1)S(1)}, bf16[1,144,640]{2,1,0:T(8,128)(2,1)}, u32[]{:S(2)}) copy-start(bf16[1,144,640]{2,1,0:T(8,128)(2,1)} %get-tuple-element.20) | copy-start | bytes 552964
  27.9 35.4 %copy-start.22 = (bf16[1,144,640]{2,1,0:T(8,128)(2,1)S(1)}, bf16[1,144,640]{2,1,0:T(8,128)(2,1)}, u32[]{:S(2)}) copy-start(bf16[1,144,640]{2,1,0:T(8,128)(2,1)} %get-tuple-element.21) | copy-start | bytes 552964
  27.9 38.1 %copy-start.21 = (bf16[1,144,640]{2,1,0:T(8,128)(2,1)S(1)}, bf16[1,144,640]{2,1,0:T(8,128)(2,1)}, u32[]{:S(2)}) copy-start(bf16[1,144,640]{2,1,0:T(8,128)(2,1)} %get-tuple-element.22) | copy-start | bytes 552964
  27.9 45.1 %copy-start.20 = (bf16[1,144,640]{2,1,0:T(8,128)(2,1)S(1)}, bf16[1,144,640]{2,1,0:T(8,128)(2,1)}, u32[]{:S(2)}) copy-start(bf16[1,144,640]{2,1,0:T(8,128)(2,1)} %get-tuple-element.23) | copy-start | bytes 552964
  33.1 72.2 %all-to-all-start.2 = ((bf16[4,288,640]{2,1,0:T(8,128)(2,1)}), bf16[4,288,640]{2,1,0:T(8,128)(2,1)S(1)}, u32[]{:S(2)}, u32[]{:S(2)}) async-start(bf16[4,288,640]{2,1,0:T(8,128)(2,1)} %get-tuple-element.32), calls=%async_computation.2 | async-start | bytes 2949120 | tf_op jit(solution)/shard_map/all_to_all | solution.py:331
  36.6 25.2 %collective-permute-start.19 = (bf16[1,144,640]{2,1,0:T(8,128)(2,1)S(1)}, bf16[1,144,640]{2,1,0:T(8,128)(2,1)S(1)}, u32[]{:S(2)}, u32[]{:S(2)}) collective-permute-start(bf16[1,144,640]{2,1,0:T(8,128)(2,1)S(1)} %copy-done.27), channel_id=1, source_target_pairs={{0,6},{1,7},{2,4},{3,5},{4,2},{5,3},{6,0},{7,1},{8,14},{9,15},{10,... | collective-permute-start | bytes 552968 | tf_op jit(solution)/shard_map/ppermute | solution.py:339
  38.6 24.7 %collective-permute-start.23 = (bf16[1,144,640]{2,1,0:T(8,128)(2,1)S(1)}, bf16[1,144,640]{2,1,0:T(8,128)(2,1)S(1)}, u32[]{:S(2)}, u32[]{:S(2)}) collective-permute-start(bf16[1,144,640]{2,1,0:T(8,128)(2,1)S(1)} %copy-done.26), channel_id=1, source_target_pairs={{0,7},{1,4},{2,5},{3,6},{4,3},{5,0},{6,1},{7,2},{8,15},{9,12},{10,... | collective-permute-start | bytes 552968 | tf_op jit(solution)/shard_map/ppermute | solution.py:339
  41.9 24.2 %collective-permute-start.28 = (bf16[1,144,640]{2,1,0:T(8,128)(2,1)S(1)}, bf16[1,144,640]{2,1,0:T(8,128)(2,1)S(1)}, u32[]{:S(2)}, u32[]{:S(2)}) collective-permute-start(bf16[1,144,640]{2,1,0:T(8,128)(2,1)S(1)} %copy-done.25), channel_id=1, source_target_pairs={{0,4},{1,5},{2,6},{3,7},{4,0},{5,1},{6,2},{7,3},{8,12},{9,13},{10,... | collective-permute-start | bytes 552968 | tf_op jit(solution)/shard_map/ppermute | solution.py:339
  41.9 31.2 %collective-permute-start.32 = (bf16[1,144,640]{2,1,0:T(8,128)(2,1)S(1)}, bf16[1,144,640]{2,1,0:T(8,128)(2,1)}, u32[]{:S(2)}, u32[]{:S(2)}) collective-permute-start(bf16[1,144,640]{2,1,0:T(8,128)(2,1)S(1)} %copy-done.24), channel_id=1, source_target_pairs={{0,5},{1,6},{2,7},{3,4},{4,1},{5,2},{6,3},{7,0},{8,13},{9,14},{10,... | collective-permute-start | bytes 552968 | tf_op jit(solution)/shard_map/ppermute | solution.py:339
  43.9 47.2 %collective-permute-start = (bf16[1,144,640]{2,1,0:T(8,128)(2,1)S(1)}, bf16[1,144,640]{2,1,0:T(8,128)(2,1)}, u32[]{:S(2)}, u32[]{:S(2)}) collective-permute-start(bf16[1,144,640]{2,1,0:T(8,128)(2,1)S(1)} %copy-done.23), channel_id=1, source_target_pairs={{0,4},{1,5},{2,6},{3,7},{4,0},{5,1},{6,2},{7,3},{8,12},{9,13},{10,... | collective-permute-start | bytes 552968 | tf_op jit(solution)/shard_map/ppermute | solution.py:339
  61.8 85.3 %copy-start.2 = (bf16[1,144,640]{2,1,0:T(8,128)(2,1)}, bf16[1,144,640]{2,1,0:T(8,128)(2,1)S(1)}, u32[]{:S(2)}) copy-start(bf16[1,144,640]{2,1,0:T(8,128)(2,1)S(1)} %collective-permute-done.19.refs_0_) | copy-start | bytes 552964
  61.8 55.1 %collective-permute-start.16 = (bf16[4,144,640]{2,1,0:T(8,128)(2,1)}, bf16[4,144,640]{2,1,0:T(8,128)(2,1)}, u32[]{:S(2)}, u32[]{:S(2)}) collective-permute-start(bf16[4,144,640]{2,1,0:T(8,128)(2,1)} %all-to-all-done.1.refs_0_), channel_id=1, source_target_pairs={{0,16},{8,24},{16,0},{24,8},{1,17},{9,25},{17,1},{25,9},{2,18},{10... | collective-permute-start | bytes 2211848 | tf_op jit(solution)/shard_map/ppermute | solution.py:367
  63.3 84.0 %copy-start.3 = (bf16[1,144,640]{2,1,0:T(8,128)(2,1)}, bf16[1,144,640]{2,1,0:T(8,128)(2,1)S(1)}, u32[]{:S(2)}) copy-start(bf16[1,144,640]{2,1,0:T(8,128)(2,1)S(1)} %collective-permute-done.23.refs_4_) | copy-start | bytes 552964
  63.3 29.3 %collective-permute-start.4 = (bf16[1,144,640]{2,1,0:T(8,128)(2,1)S(1)}, bf16[1,144,640]{2,1,0:T(8,128)(2,1)S(1)}, u32[]{:S(2)}, u32[]{:S(2)}) collective-permute-start(bf16[1,144,640]{2,1,0:T(8,128)(2,1)S(1)} %copy-done.22), channel_id=1, source_target_pairs={{0,5},{1,6},{2,7},{3,4},{4,1},{5,2},{6,3},{7,0},{8,13},{9,14},{10,... | collective-permute-start | bytes 552968 | tf_op jit(solution)/shard_map/ppermute | solution.py:339
  66.1 81.1 %copy-start.4 = (bf16[1,144,640]{2,1,0:T(8,128)(2,1)}, bf16[1,144,640]{2,1,0:T(8,128)(2,1)S(1)}, u32[]{:S(2)}) copy-start(bf16[1,144,640]{2,1,0:T(8,128)(2,1)S(1)} %collective-permute-done.28.refs_2_) | copy-start | bytes 552964
  66.1 27.1 %collective-permute-start.8 = (bf16[1,144,640]{2,1,0:T(8,128)(2,1)S(1)}, bf16[1,144,640]{2,1,0:T(8,128)(2,1)S(1)}, u32[]{:S(2)}, u32[]{:S(2)}) collective-permute-start(bf16[1,144,640]{2,1,0:T(8,128)(2,1)S(1)} %copy-done.21), channel_id=1, source_target_pairs={{0,6},{1,7},{2,4},{3,5},{4,2},{5,3},{6,0},{7,1},{8,14},{9,15},{10,... | collective-permute-start | bytes 552968 | tf_op jit(solution)/shard_map/ppermute | solution.py:339
  73.1 29.9 %collective-permute-start.12 = (bf16[1,144,640]{2,1,0:T(8,128)(2,1)S(1)}, bf16[1,144,640]{2,1,0:T(8,128)(2,1)S(1)}, u32[]{:S(2)}, u32[]{:S(2)}) collective-permute-start(bf16[1,144,640]{2,1,0:T(8,128)(2,1)S(1)} %copy-done.20), channel_id=1, source_target_pairs={{0,7},{1,4},{2,5},{3,6},{4,3},{5,0},{6,1},{7,2},{8,15},{9,12},{10,... | collective-permute-start | bytes 552968 | tf_op jit(solution)/shard_map/ppermute | solution.py:339
  91.1 13.4 %collective-permute-start.20 = (bf16[1,144,640]{2,1,0:T(8,128)(2,1)S(1)}, bf16[1,144,640]{2,1,0:T(8,128)(2,1)S(1)}, u32[]{:S(2)}, u32[]{:S(2)}) collective-permute-start(bf16[1,144,640]{2,1,0:T(8,128)(2,1)S(1)} %collective-permute-done.19.refs_0_), channel_id=1, source_target_pairs={{0,16},{8,24},{16,0},{24,8},{1,17},{9,25},{17,1},{25,9},{2,18},{10... | collective-permute-start | bytes 552968 | tf_op jit(solution)/shard_map/ppermute | solution.py:367
  92.7 11.9 %copy-start.10 = (bf16[1,144,640]{2,1,0:T(8,128)(2,1)}, bf16[1,144,640]{2,1,0:T(8,128)(2,1)S(1)}, u32[]{:S(2)}) copy-start(bf16[1,144,640]{2,1,0:T(8,128)(2,1)S(1)} %collective-permute-done.4.refs_4_) | copy-start | bytes 552964
  92.7 12.5 %collective-permute-start.24 = (bf16[1,144,640]{2,1,0:T(8,128)(2,1)S(1)}, bf16[1,144,640]{2,1,0:T(8,128)(2,1)}, u32[]{:S(2)}, u32[]{:S(2)}) collective-permute-start(bf16[1,144,640]{2,1,0:T(8,128)(2,1)S(1)} %collective-permute-done.23.refs_4_), channel_id=1, source_target_pairs={{0,16},{8,24},{16,0},{24,8},{1,17},{9,25},{17,1},{25,9},{2,18},{10... | collective-permute-start | bytes 552968 | tf_op jit(solution)/shard_map/ppermute | solution.py:367
  93.2 11.4 %copy-start.11 = (bf16[1,144,640]{2,1,0:T(8,128)(2,1)}, bf16[1,144,640]{2,1,0:T(8,128)(2,1)S(1)}, u32[]{:S(2)}) copy-start(bf16[1,144,640]{2,1,0:T(8,128)(2,1)S(1)} %collective-permute-done.8.refs_8_) | copy-start | bytes 552964
  93.2 12.1 %collective-permute-start.30 = (bf16[1,144,640]{2,1,0:T(8,128)(2,1)S(1)}, bf16[1,144,640]{2,1,0:T(8,128)(2,1)}, u32[]{:S(2)}, u32[]{:S(2)}) collective-permute-start(bf16[1,144,640]{2,1,0:T(8,128)(2,1)S(1)} %collective-permute-done.28.refs_2_), channel_id=1, source_target_pairs={{0,8},{8,0},{16,24},{24,16},{1,9},{9,1},{17,25},{25,17},{2,10},{10... | collective-permute-start | bytes 552968 | tf_op jit(solution)/shard_map/ppermute | solution.py:369
  103.0 1.6 copy-start.12
  103.0 5.6 %collective-permute-start.29 = (bf16[1,144,640]{2,1,0:T(8,128)(2,1)S(1)}, bf16[1,144,640]{2,1,0:T(8,128)(2,1)}, u32[]{:S(2)}, u32[]{:S(2)}) collective-permute-start(bf16[1,144,640]{2,1,0:T(8,128)(2,1)S(1)} %collective-permute-done.28.refs_2_), channel_id=1, source_target_pairs={{0,16},{8,24},{16,0},{24,8},{1,17},{9,25},{17,1},{25,9},{2,18},{10... | collective-permute-start | bytes 552968 | tf_op jit(solution)/shard_map/ppermute | solution.py:367
  104.5 0.7 copy-start.5
  104.5 4.1 %collective-permute-start.34 = (bf16[1,144,640]{2,1,0:T(8,128)(2,1)}, bf16[1,144,640]{2,1,0:T(8,128)(2,1)}, u32[]{:S(2)}, u32[]{:S(2)}) collective-permute-start(bf16[1,144,640]{2,1,0:T(8,128)(2,1)} %collective-permute-done.32.refs_6_), channel_id=1, source_target_pairs={{0,8},{8,0},{16,24},{24,16},{1,9},{9,1},{17,25},{25,17},{2,10},{10... | collective-permute-start | bytes 552968 | tf_op jit(solution)/shard_map/ppermute | solution.py:369
  105.2 41.9 %copy-start = (bf16[4,288,640]{2,1,0:T(8,128)(2,1)}, bf16[4,288,640]{2,1,0:T(8,128)(2,1)S(1)}, u32[]{:S(2)}) copy-start(bf16[4,288,640]{2,1,0:T(8,128)(2,1)S(1)} %all-to-all-done.2.refs_0_) | copy-start | bytes 4423684
  105.2 52.8 %collective-permute-start.27 = (bf16[4,288,640]{2,1,0:T(8,128)(2,1)S(1)}, bf16[4,288,640]{2,1,0:T(8,128)(2,1)S(1)}, u32[]{:S(2)}, u32[]{:S(2)}) collective-permute-start(bf16[4,288,640]{2,1,0:T(8,128)(2,1)S(1)} %all-to-all-done.2.refs_0_), channel_id=1, source_target_pairs={{0,8},{8,0},{16,24},{24,16},{1,9},{9,1},{17,25},{25,17},{2,10},{10... | collective-permute-start | bytes 4423688 | tf_op jit(solution)/shard_map/ppermute | solution.py:411
  105.3 7.2 %collective-permute-start.33 = (bf16[1,144,640]{2,1,0:T(8,128)(2,1)}, bf16[1,144,640]{2,1,0:T(8,128)(2,1)S(1)}, u32[]{:S(2)}, u32[]{:S(2)}) collective-permute-start(bf16[1,144,640]{2,1,0:T(8,128)(2,1)} %collective-permute-done.32.refs_6_), channel_id=1, source_target_pairs={{0,16},{8,24},{16,0},{24,8},{1,17},{9,25},{17,1},{25,9},{2,18},{10... | collective-permute-start | bytes 552968 | tf_op jit(solution)/shard_map/ppermute | solution.py:367
  108.6 3.9 %collective-permute-start.2 = (bf16[1,144,640]{2,1,0:T(8,128)(2,1)}, bf16[1,144,640]{2,1,0:T(8,128)(2,1)S(1)}, u32[]{:S(2)}, u32[]{:S(2)}) collective-permute-start(bf16[1,144,640]{2,1,0:T(8,128)(2,1)} %collective-permute-done.refs_0_), channel_id=1, source_target_pairs={{0,8},{8,0},{16,24},{24,16},{1,9},{9,1},{17,25},{25,17},{2,10},{10... | collective-permute-start | bytes 552968 | tf_op jit(solution)/shard_map/ppermute | solution.py:369
  108.6 8.3 %collective-permute-start.1 = (bf16[1,144,640]{2,1,0:T(8,128)(2,1)}, bf16[1,144,640]{2,1,0:T(8,128)(2,1)}, u32[]{:S(2)}, u32[]{:S(2)}) collective-permute-start(bf16[1,144,640]{2,1,0:T(8,128)(2,1)} %collective-permute-done.refs_0_), channel_id=1, source_target_pairs={{0,16},{8,24},{16,0},{24,8},{1,17},{9,25},{17,1},{25,9},{2,18},{10... | collective-permute-start | bytes 552968 | tf_op jit(solution)/shard_map/ppermute | solution.py:367
  112.6 20.8 %copy-start.6 = (bf16[1,144,640]{2,1,0:T(8,128)(2,1)}, bf16[1,144,640]{2,1,0:T(8,128)(2,1)S(1)}, u32[]{:S(2)}) copy-start(bf16[1,144,640]{2,1,0:T(8,128)(2,1)S(1)} %collective-permute-done.33.refs_7_) | copy-start | bytes 552964
  112.6 4.9 %collective-permute-start.6 = (bf16[1,144,640]{2,1,0:T(8,128)(2,1)}, bf16[1,144,640]{2,1,0:T(8,128)(2,1)S(1)}, u32[]{:S(2)}, u32[]{:S(2)}) collective-permute-start(bf16[1,144,640]{2,1,0:T(8,128)(2,1)} %copy-done.10), channel_id=1, source_target_pairs={{0,8},{8,0},{16,24},{24,16},{1,9},{9,1},{17,25},{25,17},{2,10},{10... | collective-permute-start | bytes 552968 | tf_op jit(solution)/shard_map/ppermute | solution.py:369
  112.6 16.4 %copy-start.13 = (bf16[1,144,640]{2,1,0:T(8,128)(2,1)}, bf16[1,144,640]{2,1,0:T(8,128)(2,1)S(1)}, u32[]{:S(2)}) copy-start(bf16[1,144,640]{2,1,0:T(8,128)(2,1)S(1)} %collective-permute-done.2.refs_2_) | copy-start | bytes 552964
  112.6 8.1 %collective-permute-start.5 = (bf16[1,144,640]{2,1,0:T(8,128)(2,1)}, bf16[1,144,640]{2,1,0:T(8,128)(2,1)}, u32[]{:S(2)}, u32[]{:S(2)}) collective-permute-start(bf16[1,144,640]{2,1,0:T(8,128)(2,1)} %copy-done.10), channel_id=1, source_target_pairs={{0,16},{8,24},{16,0},{24,8},{1,17},{9,25},{17,1},{25,9},{2,18},{10... | collective-permute-start | bytes 552968 | tf_op jit(solution)/shard_map/ppermute | solution.py:367
  116.9 18.6 %collective-permute-start.17 = (bf16[4,144,640]{2,1,0:T(8,128)(2,1)}, bf16[4,144,640]{2,1,0:T(8,128)(2,1)S(1)}, u32[]{:S(2)}, u32[]{:S(2)}) collective-permute-start(bf16[4,144,640]{2,1,0:T(8,128)(2,1)} %all-to-all-done.1.refs_0_), channel_id=1, source_target_pairs={{0,8},{8,0},{16,24},{24,16},{1,9},{9,1},{17,25},{25,17},{2,10},{10... | collective-permute-start | bytes 2211848 | tf_op jit(solution)/shard_map/ppermute | solution.py:369
  116.9 18.8 %collective-permute-start.18 = (bf16[4,144,640]{2,1,0:T(8,128)(2,1)}, bf16[4,144,640]{2,1,0:T(8,128)(2,1)S(1)}, u32[]{:S(2)}, u32[]{:S(2)}) collective-permute-start(bf16[4,144,640]{2,1,0:T(8,128)(2,1)} %collective-permute-done.16.refs_1_), channel_id=1, source_target_pairs={{0,8},{8,0},{16,24},{24,16},{1,9},{9,1},{17,25},{25,17},{2,10},{10... | collective-permute-start | bytes 2211848 | tf_op jit(solution)/shard_map/ppermute | solution.py:369
  117.4 11.6 %copy-start.14 = (bf16[1,144,640]{2,1,0:T(8,128)(2,1)}, bf16[1,144,640]{2,1,0:T(8,128)(2,1)S(1)}, u32[]{:S(2)}) copy-start(bf16[1,144,640]{2,1,0:T(8,128)(2,1)S(1)} %collective-permute-done.6.refs_6_) | copy-start | bytes 552964
  117.4 5.0 %collective-permute-start.10 = (bf16[1,144,640]{2,1,0:T(8,128)(2,1)}, bf16[1,144,640]{2,1,0:T(8,128)(2,1)S(1)}, u32[]{:S(2)}, u32[]{:S(2)}) collective-permute-start(bf16[1,144,640]{2,1,0:T(8,128)(2,1)} %copy-done.11), channel_id=1, source_target_pairs={{0,8},{8,0},{16,24},{24,16},{1,9},{9,1},{17,25},{25,17},{2,10},{10... | collective-permute-start | bytes 552968 | tf_op jit(solution)/shard_map/ppermute | solution.py:369
  120.7 6.8 %collective-permute-start.9 = (bf16[1,144,640]{2,1,0:T(8,128)(2,1)}, bf16[1,144,640]{2,1,0:T(8,128)(2,1)}, u32[]{:S(2)}, u32[]{:S(2)}) collective-permute-start(bf16[1,144,640]{2,1,0:T(8,128)(2,1)} %copy-done.11), channel_id=1, source_target_pairs={{0,16},{8,24},{16,0},{24,8},{1,17},{9,25},{17,1},{25,9},{2,18},{10... | collective-permute-start | bytes 552968 | tf_op jit(solution)/shard_map/ppermute | solution.py:367
  122.4 13.1 %copy-start.15 = (bf16[1,144,640]{2,1,0:T(8,128)(2,1)}, bf16[1,144,640]{2,1,0:T(8,128)(2,1)S(1)}, u32[]{:S(2)}) copy-start(bf16[1,144,640]{2,1,0:T(8,128)(2,1)S(1)} %collective-permute-done.10.refs_10_) | copy-start | bytes 552964
  122.4 6.5 %collective-permute-start.14 = (bf16[1,144,640]{2,1,0:T(8,128)(2,1)}, bf16[1,144,640]{2,1,0:T(8,128)(2,1)S(1)}, u32[]{:S(2)}, u32[]{:S(2)}) collective-permute-start(bf16[1,144,640]{2,1,0:T(8,128)(2,1)} %copy-done.12), channel_id=1, source_target_pairs={{0,8},{8,0},{16,24},{24,16},{1,9},{9,1},{17,25},{25,17},{2,10},{10... | collective-permute-start | bytes 552968 | tf_op jit(solution)/shard_map/ppermute | solution.py:369
  127.5 5.9 %collective-permute-start.13 = (bf16[1,144,640]{2,1,0:T(8,128)(2,1)}, bf16[1,144,640]{2,1,0:T(8,128)(2,1)}, u32[]{:S(2)}, u32[]{:S(2)}) collective-permute-start(bf16[1,144,640]{2,1,0:T(8,128)(2,1)} %copy-done.12), channel_id=1, source_target_pairs={{0,16},{8,24},{16,0},{24,8},{1,17},{9,25},{17,1},{25,9},{2,18},{10... | collective-permute-start | bytes 552968 | tf_op jit(solution)/shard_map/ppermute | solution.py:367
  128.9 6.8 %copy-start.16 = (bf16[1,144,640]{2,1,0:T(8,128)(2,1)}, bf16[1,144,640]{2,1,0:T(8,128)(2,1)S(1)}, u32[]{:S(2)}) copy-start(bf16[1,144,640]{2,1,0:T(8,128)(2,1)S(1)} %collective-permute-done.14.refs_14_) | copy-start | bytes 552964
  128.9 4.5 %collective-permute-start.31 = (bf16[1,144,640]{2,1,0:T(8,128)(2,1)}, bf16[1,144,640]{2,1,0:T(8,128)(2,1)S(1)}, u32[]{:S(2)}, u32[]{:S(2)}) collective-permute-start(bf16[1,144,640]{2,1,0:T(8,128)(2,1)} %collective-permute-done.29.refs_3_), channel_id=1, source_target_pairs={{0,8},{8,0},{16,24},{24,16},{1,9},{9,1},{17,25},{25,17},{2,10},{10... | collective-permute-start | bytes 552968 | tf_op jit(solution)/shard_map/ppermute | solution.py:369
  133.4 1.4 collective-permute-start.35
  133.4 1.4 copy-start.7
  133.4 13.7 %collective-permute-start.3 = (bf16[1,144,640]{2,1,0:T(8,128)(2,1)}, bf16[1,144,640]{2,1,0:T(8,128)(2,1)}, u32[]{:S(2)}, u32[]{:S(2)}) collective-permute-start(bf16[1,144,640]{2,1,0:T(8,128)(2,1)} %collective-permute-done.1.refs_1_), channel_id=1, source_target_pairs={{0,8},{8,0},{16,24},{24,16},{1,9},{9,1},{17,25},{25,17},{2,10},{10... | collective-permute-start | bytes 552968 | tf_op jit(solution)/shard_map/ppermute | solution.py:369
  134.8 12.5 %collective-permute-start.7 = (bf16[1,144,640]{2,1,0:T(8,128)(2,1)}, bf16[1,144,640]{2,1,0:T(8,128)(2,1)}, u32[]{:S(2)}, u32[]{:S(2)}) collective-permute-start(bf16[1,144,640]{2,1,0:T(8,128)(2,1)} %collective-permute-done.5.refs_5_), channel_id=1, source_target_pairs={{0,8},{8,0},{16,24},{24,16},{1,9},{9,1},{17,25},{25,17},{2,10},{10... | collective-permute-start | bytes 552968 | tf_op jit(solution)/shard_map/ppermute | solution.py:369
  135.5 0.9 copy-start.18
  135.5 12.2 %collective-permute-start.11 = (bf16[1,144,640]{2,1,0:T(8,128)(2,1)}, bf16[1,144,640]{2,1,0:T(8,128)(2,1)}, u32[]{:S(2)}, u32[]{:S(2)}) collective-permute-start(bf16[1,144,640]{2,1,0:T(8,128)(2,1)} %collective-permute-done.9.refs_9_), channel_id=1, source_target_pairs={{0,8},{8,0},{16,24},{24,16},{1,9},{9,1},{17,25},{25,17},{2,10},{10... | collective-permute-start | bytes 552968 | tf_op jit(solution)/shard_map/ppermute | solution.py:369
  136.4 0.9 copy-start.19
  136.4 11.5 %collective-permute-start.15 = (bf16[1,144,640]{2,1,0:T(8,128)(2,1)}, bf16[1,144,640]{2,1,0:T(8,128)(2,1)}, u32[]{:S(2)}, u32[]{:S(2)}) collective-permute-start(bf16[1,144,640]{2,1,0:T(8,128)(2,1)} %collective-permute-done.13.refs_13_), channel_id=1, source_target_pairs={{0,8},{8,0},{16,24},{24,16},{1,9},{9,1},{17,25},{25,17},{2,10},{10... | collective-permute-start | bytes 552968 | tf_op jit(solution)/shard_map/ppermute | solution.py:369
  147.2 15.6 %collective-permute-start.21 = (bf16[1,144,640]{2,1,0:T(8,128)(2,1)S(1)}, bf16[1,144,640]{2,1,0:T(8,128)(2,1)S(1)}, u32[]{:S(2)}, u32[]{:S(2)}) collective-permute-start(bf16[1,144,640]{2,1,0:T(8,128)(2,1)S(1)} %collective-permute-done.19.refs_0_), channel_id=1, source_target_pairs={{0,8},{8,0},{16,24},{24,16},{1,9},{9,1},{17,25},{25,17},{2,10},{10... | collective-permute-start | bytes 552968 | tf_op jit(solution)/shard_map/ppermute | solution.py:369
  147.4 15.4 %collective-permute-start.25 = (bf16[1,144,640]{2,1,0:T(8,128)(2,1)S(1)}, bf16[1,144,640]{2,1,0:T(8,128)(2,1)}, u32[]{:S(2)}, u32[]{:S(2)}) collective-permute-start(bf16[1,144,640]{2,1,0:T(8,128)(2,1)S(1)} %collective-permute-done.23.refs_4_), channel_id=1, source_target_pairs={{0,8},{8,0},{16,24},{24,16},{1,9},{9,1},{17,25},{25,17},{2,10},{10... | collective-permute-start | bytes 552968 | tf_op jit(solution)/shard_map/ppermute | solution.py:369
  147.7 15.1 %collective-permute-start.22 = (bf16[1,144,640]{2,1,0:T(8,128)(2,1)}, bf16[1,144,640]{2,1,0:T(8,128)(2,1)}, u32[]{:S(2)}, u32[]{:S(2)}) collective-permute-start(bf16[1,144,640]{2,1,0:T(8,128)(2,1)} %copy-done.5), channel_id=1, source_target_pairs={{0,8},{8,0},{16,24},{24,16},{1,9},{9,1},{17,25},{25,17},{2,10},{10... | collective-permute-start | bytes 552968 | tf_op jit(solution)/shard_map/ppermute | solution.py:369
  147.9 14.9 %collective-permute-start.26 = (bf16[1,144,640]{2,1,0:T(8,128)(2,1)}, bf16[1,144,640]{2,1,0:T(8,128)(2,1)}, u32[]{:S(2)}, u32[]{:S(2)}) collective-permute-start(bf16[1,144,640]{2,1,0:T(8,128)(2,1)} %collective-permute-done.24.refs_5_), channel_id=1, source_target_pairs={{0,8},{8,0},{16,24},{24,16},{1,9},{9,1},{17,25},{25,17},{2,10},{10... | collective-permute-start | bytes 552968 | tf_op jit(solution)/shard_map/ppermute | solution.py:369
  158.1 1.1 copy-start.1
  (3 other events, 2.0 us)
where the time goes:
time: 167 us
  waiting for transfers between devices  66 us (40%)
  starting transfers between devices  58.9 us (35%)
  Pallas kernels  35 us (21%)
  local copies, waits for them, and re-layouts  5.6 us (3%)
    ppermute x8, waiting for transfers between devices, far_shift(): return lax.ppermute(x, 'cache', hop)  34.5 us
    ppermute x8, starting transfers between devices, far_shift(): return lax.ppermute(x, 'cache', hop)  28.2 us
    pallas_call x2, Pallas kernels, attend_some(): pl.pallas_call(functools.partial(attend_kernel, groups, len(outs)), grid_...  19.7 us
    ppermute x9, waiting for transfers between devices, spread(): held.append(lax.ppermute(part, 'tok', hop))  19.6 us
    ppermute x9, starting transfers between devices, spread(): held.append(lax.ppermute(part, 'tok', hop))  12.8 us
    all_to_all x2, starting transfers between devices, near_exchange(): lax.all_to_all(x, 'cache', split_axis=0, concat_axis=0, tiled=True, axis_...  7.76 us
    pallas_call x2, Pallas kernels, take_rows(): pl.pallas_call(functools.partial(take_kernel, plan, count // 2, moves), o...  7.43 us
    all_to_all x1, starting transfers between devices, program(): lax.all_to_all(told, 'cache', split_axis=0, concat_axis=0, tiled=True)  7.28 us
  transfers between devices with their start and end apart: 39, of which 14 were waited for; matrix products, arithmetic and copies ran while one was open for 0% of the time, Pallas kernels for 16%

commit v1 on v0

--- a/solution.py
+++ b/solution.py
@@ -11,7 +11,7 @@
 LAT = 512
 CORES = 2
 ROWS = 16
-LATE = 2
+LATE = 3
 
 score_factor = 192.0 ** (-0.5)
 log2_e = 1.4426950408889634
@@ -206,8 +206,15 @@
 
 def attend_kernel(groups, kept, meta_ref, heard_ref, first_ref, accept_ref, row_ref, *refs):
     parts = refs[: len(groups)]
-    q1_hbm, q2_hbm, k1_ref, k2_ref = refs[len(groups) : len(groups) + 4]
-    o1_ref, o2_ref, held, q1_held, q2_held, sems, q_sems = refs[len(groups) + 4 + kept :]
+    q1_hbm, q2_hbm, *keys_hbm = refs[len(groups) : len(groups) + 4]
+    o1_ref, o2_ref, held, q1_held, q2_held, keys_ref, sems, q_sems, k_sems = refs[
+        len(groups) + 4 + kept :
+    ]
+    own_keys = keys_ref.shape[0] // 2
+    key_copies = [
+        pltpu.make_async_copy(src, keys_ref.at[pl.ds(k * own_keys, own_keys)], k_sems.at[k])
+        for k, src in enumerate(keys_hbm)
+    ]
     step = pl.program_id(0)
     base_slot = groups[0][0]
 
@@ -229,12 +236,17 @@
                 )
                 loads.append((slot, copy))
         loads.sort(key=lambda load: load[0])
+        for copy in key_copies:
+            copy.start()
         for index in range(held.shape[0]):
             for copy in query_copies(index):
                 copy.start()
             for slot, copy in loads:
                 if slot == index:
                     copy.start()
+
+        for copy in key_copies:
+            copy.wait()
 
     for copy in query_copies(step):
         copy.wait()
@@ -248,9 +260,9 @@
 
     rows = q1_held.shape[1]
     reqs = first_ref.shape[0]
-    draft = k1_ref.shape[0] // reqs
+    draft = own_keys // reqs
     heads = rows // draft
-    keys = jnp.concatenate([k1_ref[...], k2_ref[...]], axis=0)
+    keys = keys_ref[...]
     row = lax.broadcasted_iota(jnp.int32, (2 * rows, 1), 0)
     col = lax.broadcasted_iota(jnp.int32, (1, keys.shape[0]), 1)
     key = lax.div(col, reqs)
@@ -276,7 +288,6 @@
     positions = parts[0].shape[2]
     each = sum(part.shape[0] for part in parts) // count
     block = lambda lanes: pl.BlockSpec((1, rows, lanes), lambda r, *refs: (refs[4][r], 0, 0))
-    whole = pl.BlockSpec(k1.shape, lambda r, *_: (0, 0))
     out = jax.ShapeDtypeStruct((reqs, rows, LAT), jnp.bfloat16)
     flops = 2 * 2 * count * rows * positions * (width + LAT)
     start = 5 + len(parts) + 4
@@ -286,15 +297,17 @@
             num_scalar_prefetch=5,
             grid=(count,),
             in_specs=[ANY] * len(parts)
-            + [ANY, ANY, whole, whole]
+            + [ANY] * 4
             + [ANY] * len(outs),
             out_specs=[block(LAT), block(LAT)],
             scratch_shapes=[
                 pltpu.VMEM((count, width, positions), jnp.bfloat16),
                 pltpu.VMEM((count, rows, width), jnp.bfloat16),
                 pltpu.VMEM((count, rows, width), jnp.bfloat16),
+                pltpu.VMEM((2 * k1.shape[0], width), jnp.bfloat16),
                 pltpu.SemaphoreType.DMA((count, each)),
                 pltpu.SemaphoreType.DMA((count, 2)),
+                pltpu.SemaphoreType.DMA((2,)),
             ],
         ),
         out_shape=(out, out),

time: 167 us -> 174 us (1.042)
  waiting for transfers between devices: 66 us -> 90 us
  starting transfers between devices: 58.9 us -> 42.5 us
    ppermute x8, waiting for transfers between devices: 34.5 us -> 52.9 us  [far_shift(): return lax.ppermute(x, 'cache', hop)]
    ppermute x8, starting transfers between devices: 28.2 us -> 11.4 us  [far_shift(): return lax.ppermute(x, 'cache', hop)]
    ppermute x9, waiting for transfers between devices: 19.6 us -> 26.1 us  [spread(): held.append(lax.ppermute(part, 'tok', hop))]
    unnamed x56 -> x62, local copies, waits for them, and re-layouts: 5 us -> 4.55 us
  transfers between devices with their start and end apart: 39 -> 39, of which waited for: 14 -> 13; matrix products, arithmetic and copies ran while one was open for 0% -> 0% of each run, Pallas kernels for 16% -> 15%
where the time goes in v1:
time: 174 us; the launch traced here: 173 us
  waiting for transfers between devices  90 us (52%)
  starting transfers between devices  42.5 us (24%)
  Pallas kernels  34.4 us (20%)
  local copies, waits for them, and re-layouts  5.22 us (3%)
    ppermute x8, waiting for transfers between devices, far_shift(): return lax.ppermute(x, 'cache', hop)  52.9 us
    ppermute x9, waiting for transfers between devices, spread(): held.append(lax.ppermute(part, 'tok', hop))  26.1 us
    pallas_call x2, Pallas kernels, attend_some(): pl.pallas_call(functools.partial(attend_kernel, groups, len(outs)), grid_...  19.3 us
    ppermute x9, starting transfers between devices, spread(): held.append(lax.ppermute(part, 'tok', hop))  12.8 us
    ppermute x8, starting transfers between devices, far_shift(): return lax.ppermute(x, 'cache', hop)  11.4 us
    all_to_all x2, starting transfers between devices, near_exchange(): lax.all_to_all(x, 'cache', split_axis=0, concat_axis=0, tiled=True, axis_...  7.76 us
    pallas_call x2, Pallas kernels, take_rows(): pl.pallas_call(functools.partial(take_kernel, plan, count // 2, moves), o...  7.4 us
    all_to_all x1, starting transfers between devices, program(): lax.all_to_all(told, 'cache', split_axis=0, concat_axis=0, tiled=True)  7.28 us
  transfers between devices with their start and end apart: 39, of which 13 were waited for; matrix products, arithmetic and copies ran while one was open for 0% of the time, Pallas kernels for 15%

profile of v1, /device:TPU:0, one launch (start us, length us, event | category | flops | bytes accessed | tf_op | source)
XLA Modules:
  0.0 173.2 jit_solution(9938762153963619811)
XLA Ops:
  0.6 1.3 tell.1
  1.9 7.3 %all-to-all-start = ((s32[8,1,24]{2,1,0:T(1,128)}), s32[8,1,24]{2,1,0:T(1,128)S(1)}, u32[]{:S(2)}, u32[]{:S(2)}) async-start(s32[8,1,24]{2,1,0:T(1,128)} %bitcast.41), calls=%async_computation | async-start | bytes 8192 | tf_op jit(solution)/shard_map/all_to_all | solution.py:355
  9.2 0.7 stack.31.meta_ref
  9.9 5.7 %all-to-all-done = s32[8,1,24]{2,1,0:T(1,128)S(1)} async-done(((s32[8,1,24]{2,1,0:T(1,128)}), s32[8,1,24]{2,1,0:T(1,128)S(1)}, u32[]{:S(2)}, u32[]{:S(2)}) %all-to-all-start) | async-done | bytes 800 | tf_op jit(solution)/shard_map/all_to_all | solution.py:355
  15.6 0.6 copy-done.22
  16.2 3.4 %take_rows.2 = (bf16[4,144,640]{2,1,0:T(8,128)(2,1)}, bf16[1,144,640]{2,1,0:T(8,128)(2,1)}, bf16[1,144,640]{2,1,0:T(8,128)(2,1)}, bf16[1,144,640]{2,1,0:T(8,128)...) custom-call(s32[7]{0:T(128)} %stack.31.meta_ref, s32[8,24]{1,0:T(8,128)} %bitcast.32, ...), custom_call_target="tpu_custom_call" | custom-call | flops 2949120 | bytes 2949120 | tf_op jit(solution)/shard_map/take_rows/pallas_call | solution.py:96
  19.6 4.2 %all-to-all-start.1 = ((bf16[4,144,640]{2,1,0:T(8,128)(2,1)}), bf16[4,144,640]{2,1,0:T(8,128)(2,1)}, u32[]{:S(2)}, u32[]{:S(2)}) async-start(bf16[4,144,640]{2,1,0:T(8,128)(2,1)} %get-tuple-element.25), calls=%async_computation.1 | async-start | bytes 1474560 | tf_op jit(solution)/shard_map/all_to_all | solution.py:344
  23.8 4.0 %take_rows.3 = (bf16[4,288,640]{2,1,0:T(8,128)(2,1)}, bf16[1,144,640]{2,1,0:T(8,128)(2,1)}, bf16[1,144,640]{2,1,0:T(8,128)(2,1)}, bf16[1,144,640]{2,1,0:T(8,128)(2,1)}, bf16[1,144,640]{2,1,0:T(8,128)(2,1)}) custom-call(s32[7]{0:T(128)} %stack.31.meta_ref, s32[8]{0:T(128)} %move_ref.5, bf16[8,576,640]{2,1,0:T(8,128)(2,1)} %bitcast.24), custom_call_target="tpu_custom_call" | custom-call | flops 4423680 | bytes 4423680 | tf_op jit(solution)/shard_map/take_rows/pallas_call | solution.py:96
  27.9 0.0 copy-start.26
  27.9 5.1 %all-to-all-done.1.refs_0_ = bf16[4,144,640]{2,1,0:T(8,128)(2,1)} async-done(((bf16[4,144,640]{2,1,0:T(8,128)(2,1)}), bf16[4,144,640]{2,1,0:T(8,128)(2,1)}, u32[]{:S(2)}, u32[]{:S(2)}) %all-to-all-start.1) | async-done | bytes 737312 | tf_op jit(solution)/shard_map/all_to_all | solution.py:344
  33.1 3.6 %all-to-all-start.2 = ((bf16[4,288,640]{2,1,0:T(8,128)(2,1)}), bf16[4,288,640]{2,1,0:T(8,128)(2,1)S(1)}, u32[]{:S(2)}, u32[]{:S(2)}) async-start(bf16[4,288,640]{2,1,0:T(8,128)(2,1)} %get-tuple-element.33), calls=%async_computation.2 | async-start | bytes 2949120 | tf_op jit(solution)/shard_map/all_to_all | solution.py:344
  36.6 2.0 %collective-permute-start.19 = (bf16[1,144,640]{2,1,0:T(8,128)(2,1)S(1)}, bf16[1,144,640]{2,1,0:T(8,128)(2,1)S(1)}, u32[]{:S(2)}, u32[]{:S(2)}) collective-permute-start(bf16[1,144,640]{2,1,0:T(8,128)(2,1)S(1)} %copy-done.30), channel_id=1, source_target_pairs={{0,5},{1,6},{2,7},{3,4},{4,1},{5,2},{6,3},{7,0},{8,13},{9,14},{10,... | collective-permute-start | bytes 552968 | tf_op jit(solution)/shard_map/ppermute | solution.py:352
  38.6 3.3 %collective-permute-start.23 = (bf16[1,144,640]{2,1,0:T(8,128)(2,1)S(1)}, bf16[1,144,640]{2,1,0:T(8,128)(2,1)S(1)}, u32[]{:S(2)}, u32[]{:S(2)}) collective-permute-start(bf16[1,144,640]{2,1,0:T(8,128)(2,1)S(1)} %copy-done.29), channel_id=1, source_target_pairs={{0,6},{1,7},{2,4},{3,5},{4,2},{5,3},{6,0},{7,1},{8,14},{9,15},{10,... | collective-permute-start | bytes 552968 | tf_op jit(solution)/shard_map/ppermute | solution.py:352
  41.9 1.5 collective-permute-start.27
  43.3 0.0 collective-permute-start.32
  43.3 2.9 %collective-permute-start = (bf16[1,144,640]{2,1,0:T(8,128)(2,1)S(1)}, bf16[1,144,640]{2,1,0:T(8,128)(2,1)S(1)}, u32[]{:S(2)}, u32[]{:S(2)}) collective-permute-start(bf16[1,144,640]{2,1,0:T(8,128)(2,1)S(1)} %copy-done.26), channel_id=1, source_target_pairs={{0,4},{1,5},{2,6},{3,7},{4,0},{5,1},{6,2},{7,3},{8,12},{9,13},{10,... | collective-permute-start | bytes 552968 | tf_op jit(solution)/shard_map/ppermute | solution.py:352
  46.3 18.4 %collective-permute-done.19.refs_0_ = bf16[1,144,640]{2,1,0:T(8,128)(2,1)S(1)} collective-permute-done((bf16[1,144,640]{2,1,0:T(8,128)(2,1)S(1)}, bf16[1,144,640]{2,1,0:T(8,128)(2,1)S(1)}, u32[]{:S(2)}, u32[]{:S(2)}) %collective-permute-start.19) | collective-permute-done | bytes 184352 | tf_op jit(solution)/shard_map/ppermute | solution.py:352
  64.7 1.5 collective-permute-start.16
  66.2 0.1 collective-permute-start.4
  66.3 1.7 collective-permute-start.8
  68.0 19.9 %collective-permute-done.32.refs_2_ = bf16[1,144,640]{2,1,0:T(8,128)(2,1)S(1)} collective-permute-done((bf16[1,144,640]{2,1,0:T(8,128)(2,1)S(1)}, bf16[1,144,640]{2,1,0:T(8,128)(2,1)S(1)}, u32[]{:S(2)}, u32[]{:S(2)}) %collective-permute-start.32) | collective-permute-done | bytes 184352 | tf_op jit(solution)/shard_map/ppermute | solution.py:352
  87.9 3.9 %collective-permute-done.refs_0_ = bf16[1,144,640]{2,1,0:T(8,128)(2,1)S(1)} collective-permute-done((bf16[1,144,640]{2,1,0:T(8,128)(2,1)S(1)}, bf16[1,144,640]{2,1,0:T(8,128)(2,1)S(1)}, u32[]{:S(2)}, u32[]{:S(2)}) %collective-permute-start) | collective-permute-done | bytes 184352 | tf_op jit(solution)/shard_map/ppermute | solution.py:352
  91.9 0.7 copy-done.9
  92.6 0.7 copy-done.11
  93.3 1.6 collective-permute-start.20
  94.8 10.6 %collective-permute-done.12.refs_12_ = bf16[1,144,640]{2,1,0:T(8,128)(2,1)} collective-permute-done((bf16[1,144,640]{2,1,0:T(8,128)(2,1)}, bf16[1,144,640]{2,1,0:T(8,128)(2,1)}, u32[]{:S(2)}, u32[]{:S(2)}) %collective-permute-start.12) | collective-permute-done | bytes 184352 | tf_op jit(solution)/shard_map/ppermute | solution.py:352
  105.4 1.5 collective-permute-start.24
  107.0 0.5 collective-permute-start.28
  107.5 0.1 collective-permute-start.34
  107.6 5.4 %collective-permute-done.24.refs_5_ = bf16[1,144,640]{2,1,0:T(8,128)(2,1)S(1)} collective-permute-done((bf16[1,144,640]{2,1,0:T(8,128)(2,1)S(1)}, bf16[1,144,640]{2,1,0:T(8,128)(2,1)S(1)}, u32[]{:S(2)}, u32[]{:S(2)}) %collective-permute-start.24) | collective-permute-done | bytes 184352 | tf_op jit(solution)/shard_map/ppermute | solution.py:380
  112.9 1.5 collective-permute-start.33
  114.5 2.1 %collective-permute-done.28.refs_9_ = bf16[1,144,640]{2,1,0:T(8,128)(2,1)S(1)} collective-permute-done((bf16[1,144,640]{2,1,0:T(8,128)(2,1)}, bf16[1,144,640]{2,1,0:T(8,128)(2,1)S(1)}, u32[]{:S(2)}, u32[]{:S(2)}) %collective-permute-start.28) | collective-permute-done | bytes 184352 | tf_op jit(solution)/shard_map/ppermute | solution.py:380
  116.6 1.6 collective-permute-start.1
  118.2 0.4 collective-permute-done.33.refs_3_
  118.5 0.5 collective-permute-start.17
  119.0 0.1 collective-permute-start.18
  119.1 4.8 %collective-permute-done.1.refs_1_ = bf16[1,144,640]{2,1,0:T(8,128)(2,1)} collective-permute-done((bf16[1,144,640]{2,1,0:T(8,128)(2,1)}, bf16[1,144,640]{2,1,0:T(8,128)(2,1)}, u32[]{:S(2)}, u32[]{:S(2)}) %collective-permute-start.1) | collective-permute-done | bytes 184352 | tf_op jit(solution)/shard_map/ppermute | solution.py:380
  123.9 1.5 collective-permute-start.5
  125.5 4.9 %collective-permute-done.5.refs_5_ = bf16[1,144,640]{2,1,0:T(8,128)(2,1)} collective-permute-done((bf16[1,144,640]{2,1,0:T(8,128)(2,1)}, bf16[1,144,640]{2,1,0:T(8,128)(2,1)}, u32[]{:S(2)}, u32[]{:S(2)}) %collective-permute-start.5) | collective-permute-done | bytes 184352 | tf_op jit(solution)/shard_map/ppermute | solution.py:380
  130.4 1.5 collective-permute-start.9
  131.9 4.3 %collective-permute-done.9.refs_9_ = bf16[1,144,640]{2,1,0:T(8,128)(2,1)} collective-permute-done((bf16[1,144,640]{2,1,0:T(8,128)(2,1)}, bf16[1,144,640]{2,1,0:T(8,128)(2,1)}, u32[]{:S(2)}, u32[]{:S(2)}) %collective-permute-start.9) | collective-permute-done | bytes 184352 | tf_op jit(solution)/shard_map/ppermute | solution.py:380
  136.2 1.5 collective-permute-start.13
  137.7 0.1 collective-permute-start.35
  137.8 4.3 %collective-permute-done.13.refs_13_ = bf16[1,144,640]{2,1,0:T(8,128)(2,1)} collective-permute-done((bf16[1,144,640]{2,1,0:T(8,128)(2,1)}, bf16[1,144,640]{2,1,0:T(8,128)(2,1)}, u32[]{:S(2)}, u32[]{:S(2)}) %collective-permute-start.13) | collective-permute-done | bytes 184352 | tf_op jit(solution)/shard_map/ppermute | solution.py:380
  142.1 0.7 copy-done.5
  142.7 0.5 collective-permute-start.7
  143.3 0.0 copy-start.23
  143.3 0.1 collective-permute-start.11
  143.4 0.5 collective-permute-start.15
  143.9 0.2 copy-done.23
  144.1 0.2 copy-done.24
  144.4 9.6 %attend_some.2 = (bf16[8,192,512]{2,1,0:T(8,128)(2,1)}, bf16[8,192,512]{2,1,0:T(8,128)(2,1)}) custom-call(s32[7]{0:T(128)} %stack.31.meta_ref, s32[8,24]{1,0:T(8,128)} %bitcast.33, s32[8]{0:T(128)} %first_ref.5, s32[8]{0:T(128)} %accept_ref.3, s32[4]{0:T(128)} %get-tuple-element.24.row_ref, bf16[4,144,640]{2,1,0:T(8,128)(2,1)} %all-to-all-done.1.refs_0_, ...), custom_call_target="tpu_custom_call" | custom-call | flops 2139095040 | bytes 5898240 | tf_op jit(solution)/shard_map/attend_some/pallas_call | solution.py:294
  154.0 0.4 collective-permute-start.25
  154.5 0.2 collective-permute-start.29
  154.6 0.4 collective-permute-start.22
  155.0 0.2 collective-permute-start.26
  155.1 0.4 collective-permute-start.30
  155.5 9.7 %attend_some.3 = (bf16[8,192,512]{2,1,0:T(8,128)(2,1)}, bf16[8,192,512]{2,1,0:T(8,128)(2,1)}) custom-call(s32[7]{0:T(128)} %stack.31.meta_ref, s32[8,24]{1,0:T(8,128)} %bitcast.34, s32[8]{0:T(128)} %first_ref.5, s32[8]{0:T(128)} %accept_ref.3, s32[4]{0:T(128)} %get-tuple-element.19.row_ref, ...), custom_call_target="tpu_custom_call", output_to_operand_aliasing={{0}: (25, {}), {1}: (26, {})} | custom-call | flops 2139095040 | bytes 5898240 | tf_op jit(solution)/shard_map/attend_some/pallas_call | solution.py:294
  165.2 3.1 %place_parts.2.refs_12_ = bf16[4,576,640]{2,1,0:T(8,128)(2,1)} custom-call(s32[7]{0:T(128)} %stack.31.meta_ref, s32[8,24]{1,0:T(8,128)} %bitcast.35, s32[8]{0:T(128)} %move_ref.5, bf16[4,288,640]{2,1,0:T(8,128)(2,1)} %copy-done, bf16[4,288,640]{2,1,0:T(8,128)(2,1)} %copy-done.1, bf16[1,144,640]{2,1,0:T(8,128)(2,1)} %copy-done.2, ...), custom_call_target="tpu_custom_call" | custom-call | flops 2949120 | bytes 2949120 | tf_op jit(solution)/shard_map/place_parts/pallas_call | solution.py:162
  168.4 0.6 copy-done.18
  169.0 0.0 copy-done.19
  169.1 0.1 copy-done.20
  169.1 0.7 copy-done.21
  169.8 3.3 %place_parts.3 = bf16[4,576,640]{2,1,0:T(8,128)(2,1)} custom-call(s32[7]{0:T(128)} %stack.31.meta_ref, s32[8,24]{1,0:T(8,128)} %bitcast.36, s32[8]{0:T(128)} %move_ref.5, bf16[1,144,640]{2,1,0:T(8,128)(2,1)} %copy-done.6, bf16[1,144,640]{2,1,0:T(8,128)(2,1)} %copy-done.10, ...), custom_call_target="tpu_custom_call", output_to_operand_aliasing={{}: (15, {})} | custom-call | flops 2949120 | bytes 2949120 | tf_op jit(solution)/shard_map/place_parts/pallas_call | solution.py:162
  (84 shorter events, 0.2 us)
Async XLA Ops:
  1.9 13.7 %all-to-all-start = ((s32[8,1,24]{2,1,0:T(1,128)}), s32[8,1,24]{2,1,0:T(1,128)S(1)}, u32[]{:S(2)}, u32[]{:S(2)}) async-start(s32[8,1,24]{2,1,0:T(1,128)} %bitcast.41), calls=%async_computation | async-start | bytes 8192 | tf_op jit(solution)/shard_map/all_to_all | solution.py:355
  19.6 13.4 %all-to-all-start.1 = ((bf16[4,144,640]{2,1,0:T(8,128)(2,1)}), bf16[4,144,640]{2,1,0:T(8,128)(2,1)}, u32[]{:S(2)}, u32[]{:S(2)}) async-start(bf16[4,144,640]{2,1,0:T(8,128)(2,1)} %get-tuple-element.25), calls=%async_computation.1 | async-start | bytes 1474560 | tf_op jit(solution)/shard_map/all_to_all | solution.py:344
  27.8 8.8 %copy-start.30 = (bf16[1,144,640]{2,1,0:T(8,128)(2,1)S(1)}, bf16[1,144,640]{2,1,0:T(8,128)(2,1)}, u32[]{:S(2)}) copy-start(bf16[1,144,640]{2,1,0:T(8,128)(2,1)} %get-tuple-element.30) | copy-start | bytes 552964
  27.9 10.7 %copy-start.29 = (bf16[1,144,640]{2,1,0:T(8,128)(2,1)S(1)}, bf16[1,144,640]{2,1,0:T(8,128)(2,1)}, u32[]{:S(2)}) copy-start(bf16[1,144,640]{2,1,0:T(8,128)(2,1)} %get-tuple-element.31) | copy-start | bytes 552964
  27.9 14.0 %copy-start.28 = (bf16[1,144,640]{2,1,0:T(8,128)(2,1)S(1)}, bf16[1,144,640]{2,1,0:T(8,128)(2,1)}, u32[]{:S(2)}) copy-start(bf16[1,144,640]{2,1,0:T(8,128)(2,1)} %get-tuple-element.32) | copy-start | bytes 552964
  27.9 15.5 %copy-start.27 = (bf16[1,144,640]{2,1,0:T(8,128)(2,1)S(1)}, bf16[1,144,640]{2,1,0:T(8,128)(2,1)}, u32[]{:S(2)}) copy-start(bf16[1,144,640]{2,1,0:T(8,128)(2,1)} %get-tuple-element.34) | copy-start | bytes 552964
  27.9 15.5 %copy-start.26 = (bf16[1,144,640]{2,1,0:T(8,128)(2,1)S(1)}, bf16[1,144,640]{2,1,0:T(8,128)(2,1)}, u32[]{:S(2)}) copy-start(bf16[1,144,640]{2,1,0:T(8,128)(2,1)} %get-tuple-element.20) | copy-start | bytes 552964
  27.9 38.3 %copy-start.25 = (bf16[1,144,640]{2,1,0:T(8,128)(2,1)S(1)}, bf16[1,144,640]{2,1,0:T(8,128)(2,1)}, u32[]{:S(2)}) copy-start(bf16[1,144,640]{2,1,0:T(8,128)(2,1)} %get-tuple-element.21) | copy-start | bytes 552964
  33.1 60.2 %all-to-all-start.2 = ((bf16[4,288,640]{2,1,0:T(8,128)(2,1)}), bf16[4,288,640]{2,1,0:T(8,128)(2,1)S(1)}, u32[]{:S(2)}, u32[]{:S(2)}) async-start(bf16[4,288,640]{2,1,0:T(8,128)(2,1)} %get-tuple-element.33), calls=%async_computation.2 | async-start | bytes 2949120 | tf_op jit(solution)/shard_map/all_to_all | solution.py:344
  36.6 28.1 %collective-permute-start.19 = (bf16[1,144,640]{2,1,0:T(8,128)(2,1)S(1)}, bf16[1,144,640]{2,1,0:T(8,128)(2,1)S(1)}, u32[]{:S(2)}, u32[]{:S(2)}) collective-permute-start(bf16[1,144,640]{2,1,0:T(8,128)(2,1)S(1)} %copy-done.30), channel_id=1, source_target_pairs={{0,5},{1,6},{2,7},{3,4},{4,1},{5,2},{6,3},{7,0},{8,13},{9,14},{10,... | collective-permute-start | bytes 552968 | tf_op jit(solution)/shard_map/ppermute | solution.py:352
  38.6 27.6 %collective-permute-start.23 = (bf16[1,144,640]{2,1,0:T(8,128)(2,1)S(1)}, bf16[1,144,640]{2,1,0:T(8,128)(2,1)S(1)}, u32[]{:S(2)}, u32[]{:S(2)}) collective-permute-start(bf16[1,144,640]{2,1,0:T(8,128)(2,1)S(1)} %copy-done.29), channel_id=1, source_target_pairs={{0,6},{1,7},{2,4},{3,5},{4,2},{5,3},{6,0},{7,1},{8,14},{9,15},{10,... | collective-permute-start | bytes 552968 | tf_op jit(solution)/shard_map/ppermute | solution.py:352
  41.9 24.4 %collective-permute-start.27 = (bf16[1,144,640]{2,1,0:T(8,128)(2,1)S(1)}, bf16[1,144,640]{2,1,0:T(8,128)(2,1)S(1)}, u32[]{:S(2)}, u32[]{:S(2)}) collective-permute-start(bf16[1,144,640]{2,1,0:T(8,128)(2,1)S(1)} %copy-done.28), channel_id=1, source_target_pairs={{0,7},{1,4},{2,5},{3,6},{4,3},{5,0},{6,1},{7,2},{8,15},{9,12},{10,... | collective-permute-start | bytes 552968 | tf_op jit(solution)/shard_map/ppermute | solution.py:352
  43.3 44.6 %collective-permute-start.32 = (bf16[1,144,640]{2,1,0:T(8,128)(2,1)S(1)}, bf16[1,144,640]{2,1,0:T(8,128)(2,1)S(1)}, u32[]{:S(2)}, u32[]{:S(2)}) collective-permute-start(bf16[1,144,640]{2,1,0:T(8,128)(2,1)S(1)} %copy-done.27), channel_id=1, source_target_pairs={{0,4},{1,5},{2,6},{3,7},{4,0},{5,1},{6,2},{7,3},{8,12},{9,13},{10,... | collective-permute-start | bytes 552968 | tf_op jit(solution)/shard_map/ppermute | solution.py:352
  43.3 48.5 %collective-permute-start = (bf16[1,144,640]{2,1,0:T(8,128)(2,1)S(1)}, bf16[1,144,640]{2,1,0:T(8,128)(2,1)S(1)}, u32[]{:S(2)}, u32[]{:S(2)}) collective-permute-start(bf16[1,144,640]{2,1,0:T(8,128)(2,1)S(1)} %copy-done.26), channel_id=1, source_target_pairs={{0,4},{1,5},{2,6},{3,7},{4,0},{5,1},{6,2},{7,3},{8,12},{9,13},{10,... | collective-permute-start | bytes 552968 | tf_op jit(solution)/shard_map/ppermute | solution.py:352
  64.7 42.8 %copy-start.6 = (bf16[1,144,640]{2,1,0:T(8,128)(2,1)}, bf16[1,144,640]{2,1,0:T(8,128)(2,1)S(1)}, u32[]{:S(2)}) copy-start(bf16[1,144,640]{2,1,0:T(8,128)(2,1)S(1)} %collective-permute-done.19.refs_0_) | copy-start | bytes 552964
  64.7 54.4 %collective-permute-start.16 = (bf16[4,144,640]{2,1,0:T(8,128)(2,1)}, bf16[4,144,640]{2,1,0:T(8,128)(2,1)}, u32[]{:S(2)}, u32[]{:S(2)}) collective-permute-start(bf16[4,144,640]{2,1,0:T(8,128)(2,1)} %all-to-all-done.1.refs_0_), channel_id=1, source_target_pairs={{0,16},{8,24},{16,0},{24,8},{1,17},{9,25},{17,1},{25,9},{2,18},{10... | collective-permute-start | bytes 2211848 | tf_op jit(solution)/shard_map/ppermute | solution.py:380
  66.2 41.3 %copy-start.7 = (bf16[1,144,640]{2,1,0:T(8,128)(2,1)}, bf16[1,144,640]{2,1,0:T(8,128)(2,1)S(1)}, u32[]{:S(2)}) copy-start(bf16[1,144,640]{2,1,0:T(8,128)(2,1)S(1)} %collective-permute-done.23.refs_4_) | copy-start | bytes 552964
  66.2 25.7 %collective-permute-start.4 = (bf16[1,144,640]{2,1,0:T(8,128)(2,1)S(1)}, bf16[1,144,640]{2,1,0:T(8,128)(2,1)S(1)}, u32[]{:S(2)}, u32[]{:S(2)}) collective-permute-start(bf16[1,144,640]{2,1,0:T(8,128)(2,1)S(1)} %copy-done.25), channel_id=1, source_target_pairs={{0,5},{1,6},{2,7},{3,4},{4,1},{5,2},{6,3},{7,0},{8,13},{9,14},{10,... | collective-permute-start | bytes 552968 | tf_op jit(solution)/shard_map/ppermute | solution.py:352
  66.3 25.6 %copy-start.8 = (bf16[1,144,640]{2,1,0:T(8,128)(2,1)}, bf16[1,144,640]{2,1,0:T(8,128)(2,1)S(1)}, u32[]{:S(2)}) copy-start(bf16[1,144,640]{2,1,0:T(8,128)(2,1)S(1)} %collective-permute-done.27.refs_8_) | copy-start | bytes 552964
  66.3 27.0 %collective-permute-start.8 = (bf16[1,144,640]{2,1,0:T(8,128)(2,1)}, bf16[1,144,640]{2,1,0:T(8,128)(2,1)}, u32[]{:S(2)}, u32[]{:S(2)}) collective-permute-start(bf16[1,144,640]{2,1,0:T(8,128)(2,1)} %get-tuple-element.22), channel_id=1, source_target_pairs={{0,6},{1,7},{2,4},{3,5},{4,2},{5,3},{6,0},{7,1},{8,14},{9,15},{10,... | collective-permute-start | bytes 552968 | tf_op jit(solution)/shard_map/ppermute | solution.py:352
  87.9 66.1 %copy-start.2 = (bf16[1,144,640]{2,1,0:T(8,128)(2,1)}, bf16[1,144,640]{2,1,0:T(8,128)(2,1)S(1)}, u32[]{:S(2)}) copy-start(bf16[1,144,640]{2,1,0:T(8,128)(2,1)S(1)} %collective-permute-done.32.refs_2_) | copy-start | bytes 552964
  87.9 17.5 %collective-permute-start.12 = (bf16[1,144,640]{2,1,0:T(8,128)(2,1)}, bf16[1,144,640]{2,1,0:T(8,128)(2,1)}, u32[]{:S(2)}, u32[]{:S(2)}) collective-permute-start(bf16[1,144,640]{2,1,0:T(8,128)(2,1)} %get-tuple-element.23), channel_id=1, source_target_pairs={{0,7},{1,4},{2,5},{3,6},{4,3},{5,0},{6,1},{7,2},{8,15},{9,12},{10,... | collective-permute-start | bytes 552968 | tf_op jit(solution)/shard_map/ppermute | solution.py:352
  91.9 15.1 %collective-permute-start.21 = (bf16[1,144,640]{2,1,0:T(8,128)(2,1)S(1)}, bf16[1,144,640]{2,1,0:T(8,128)(2,1)}, u32[]{:S(2)}, u32[]{:S(2)}) collective-permute-start(bf16[1,144,640]{2,1,0:T(8,128)(2,1)S(1)} %collective-permute-done.19.refs_0_), channel_id=1, source_target_pairs={{0,8},{8,0},{16,24},{24,16},{1,9},{9,1},{17,25},{25,17},{2,10},{10... | collective-permute-start | bytes 552968 | tf_op jit(solution)/shard_map/ppermute | solution.py:382
  93.2 60.8 %copy-start = (bf16[4,288,640]{2,1,0:T(8,128)(2,1)}, bf16[4,288,640]{2,1,0:T(8,128)(2,1)S(1)}, u32[]{:S(2)}) copy-start(bf16[4,288,640]{2,1,0:T(8,128)(2,1)S(1)} %all-to-all-done.2.refs_0_) | copy-start | bytes 4423684
  93.2 61.9 %collective-permute-start.31 = (bf16[4,288,640]{2,1,0:T(8,128)(2,1)S(1)}, bf16[4,288,640]{2,1,0:T(8,128)(2,1)S(1)}, u32[]{:S(2)}, u32[]{:S(2)}) collective-permute-start(bf16[4,288,640]{2,1,0:T(8,128)(2,1)S(1)} %all-to-all-done.2.refs_0_), channel_id=1, source_target_pairs={{0,8},{8,0},{16,24},{24,16},{1,9},{9,1},{17,25},{25,17},{2,10},{10... | collective-permute-start | bytes 4423688 | tf_op jit(solution)/shard_map/ppermute | solution.py:424
  93.3 14.2 %collective-permute-start.20 = (bf16[1,144,640]{2,1,0:T(8,128)(2,1)S(1)}, bf16[1,144,640]{2,1,0:T(8,128)(2,1)S(1)}, u32[]{:S(2)}, u32[]{:S(2)}) collective-permute-start(bf16[1,144,640]{2,1,0:T(8,128)(2,1)S(1)} %collective-permute-done.19.refs_0_), channel_id=1, source_target_pairs={{0,16},{8,24},{16,0},{24,8},{1,17},{9,25},{17,1},{25,9},{2,18},{10... | collective-permute-start | bytes 552968 | tf_op jit(solution)/shard_map/ppermute | solution.py:380
  105.4 7.5 %collective-permute-start.24 = (bf16[1,144,640]{2,1,0:T(8,128)(2,1)S(1)}, bf16[1,144,640]{2,1,0:T(8,128)(2,1)S(1)}, u32[]{:S(2)}, u32[]{:S(2)}) collective-permute-start(bf16[1,144,640]{2,1,0:T(8,128)(2,1)S(1)} %collective-permute-done.23.refs_4_), channel_id=1, source_target_pairs={{0,16},{8,24},{16,0},{24,8},{1,17},{9,25},{17,1},{25,9},{2,18},{10... | collective-permute-start | bytes 552968 | tf_op jit(solution)/shard_map/ppermute | solution.py:380
  107.0 9.6 %collective-permute-start.28 = (bf16[1,144,640]{2,1,0:T(8,128)(2,1)}, bf16[1,144,640]{2,1,0:T(8,128)(2,1)S(1)}, u32[]{:S(2)}, u32[]{:S(2)}) collective-permute-start(bf16[1,144,640]{2,1,0:T(8,128)(2,1)} %copy-done.8), channel_id=1, source_target_pairs={{0,16},{8,24},{16,0},{24,8},{1,17},{9,25},{17,1},{25,9},{2,18},{10... | collective-permute-start | bytes 552968 | tf_op jit(solution)/shard_map/ppermute | solution.py:380
  107.5 30.3 %copy-start.10 = (bf16[1,144,640]{2,1,0:T(8,128)(2,1)}, bf16[1,144,640]{2,1,0:T(8,128)(2,1)S(1)}, u32[]{:S(2)}) copy-start(bf16[1,144,640]{2,1,0:T(8,128)(2,1)S(1)} %collective-permute-done.20.refs_1_) | copy-start | bytes 552964
  107.5 9.1 %collective-permute-start.34 = (bf16[1,144,640]{2,1,0:T(8,128)(2,1)S(1)}, bf16[1,144,640]{2,1,0:T(8,128)(2,1)S(1)}, u32[]{:S(2)}, u32[]{:S(2)}) collective-permute-start(bf16[1,144,640]{2,1,0:T(8,128)(2,1)S(1)} %collective-permute-done.32.refs_2_), channel_id=1, source_target_pairs={{0,8},{8,0},{16,24},{24,16},{1,9},{9,1},{17,25},{25,17},{2,10},{10... | collective-permute-start | bytes 552968 | tf_op jit(solution)/shard_map/ppermute | solution.py:382
  112.9 30.3 %copy-start.12 = (bf16[1,144,640]{2,1,0:T(8,128)(2,1)}, bf16[1,144,640]{2,1,0:T(8,128)(2,1)S(1)}, u32[]{:S(2)}) copy-start(bf16[1,144,640]{2,1,0:T(8,128)(2,1)S(1)} %collective-permute-done.24.refs_5_) | copy-start | bytes 552964
  112.9 5.6 %collective-permute-start.33 = (bf16[1,144,640]{2,1,0:T(8,128)(2,1)S(1)}, bf16[1,144,640]{2,1,0:T(8,128)(2,1)S(1)}, u32[]{:S(2)}, u32[]{:S(2)}) collective-permute-start(bf16[1,144,640]{2,1,0:T(8,128)(2,1)S(1)} %collective-permute-done.32.refs_2_), channel_id=1, source_target_pairs={{0,16},{8,24},{16,0},{24,8},{1,17},{9,25},{17,1},{25,9},{2,18},{10... | collective-permute-start | bytes 552968 | tf_op jit(solution)/shard_map/ppermute | solution.py:380
  116.6 26.7 %copy-start.13 = (bf16[1,144,640]{2,1,0:T(8,128)(2,1)}, bf16[1,144,640]{2,1,0:T(8,128)(2,1)S(1)}, u32[]{:S(2)}) copy-start(bf16[1,144,640]{2,1,0:T(8,128)(2,1)S(1)} %collective-permute-done.28.refs_9_) | copy-start | bytes 552964
  116.6 2.0 %collective-permute-start.2 = (bf16[1,144,640]{2,1,0:T(8,128)(2,1)}, bf16[1,144,640]{2,1,0:T(8,128)(2,1)S(1)}, u32[]{:S(2)}, u32[]{:S(2)}) collective-permute-start(bf16[1,144,640]{2,1,0:T(8,128)(2,1)} %copy-done.9), channel_id=1, source_target_pairs={{0,8},{8,0},{16,24},{24,16},{1,9},{9,1},{17,25},{25,17},{2,10},{10... | collective-permute-start | bytes 552968 | tf_op jit(solution)/shard_map/ppermute | solution.py:382
  116.6 37.4 %copy-start.3 = (bf16[1,144,640]{2,1,0:T(8,128)(2,1)}, bf16[1,144,640]{2,1,0:T(8,128)(2,1)S(1)}, u32[]{:S(2)}) copy-start(bf16[1,144,640]{2,1,0:T(8,128)(2,1)S(1)} %collective-permute-done.34.refs_4_) | copy-start | bytes 552964
  116.6 7.4 %collective-permute-start.1 = (bf16[1,144,640]{2,1,0:T(8,128)(2,1)}, bf16[1,144,640]{2,1,0:T(8,128)(2,1)}, u32[]{:S(2)}, u32[]{:S(2)}) collective-permute-start(bf16[1,144,640]{2,1,0:T(8,128)(2,1)} %copy-done.9), channel_id=1, source_target_pairs={{0,16},{8,24},{16,0},{24,8},{1,17},{9,25},{17,1},{25,9},{2,18},{10... | collective-permute-start | bytes 552968 | tf_op jit(solution)/shard_map/ppermute | solution.py:380
  118.5 35.5 %copy-start.4 = (bf16[1,144,640]{2,1,0:T(8,128)(2,1)}, bf16[1,144,640]{2,1,0:T(8,128)(2,1)S(1)}, u32[]{:S(2)}) copy-start(bf16[1,144,640]{2,1,0:T(8,128)(2,1)S(1)} %collective-permute-done.33.refs_3_) | copy-start | bytes 552964
  118.5 6.9 %collective-permute-start.6 = (bf16[1,144,640]{2,1,0:T(8,128)(2,1)}, bf16[1,144,640]{2,1,0:T(8,128)(2,1)S(1)}, u32[]{:S(2)}, u32[]{:S(2)}) collective-permute-start(bf16[1,144,640]{2,1,0:T(8,128)(2,1)} %copy-done.11), channel_id=1, source_target_pairs={{0,8},{8,0},{16,24},{24,16},{1,9},{9,1},{17,25},{25,17},{2,10},{10... | collective-permute-start | bytes 552968 | tf_op jit(solution)/shard_map/ppermute | solution.py:382
  118.5 24.8 %copy-start.14 = (bf16[1,144,640]{2,1,0:T(8,128)(2,1)}, bf16[1,144,640]{2,1,0:T(8,128)(2,1)S(1)}, u32[]{:S(2)}) copy-start(bf16[1,144,640]{2,1,0:T(8,128)(2,1)S(1)} %collective-permute-done.2.refs_2_) | copy-start | bytes 552964
  118.5 24.7 %collective-permute-start.17 = (bf16[4,144,640]{2,1,0:T(8,128)(2,1)}, bf16[4,144,640]{2,1,0:T(8,128)(2,1)S(1)}, u32[]{:S(2)}, u32[]{:S(2)}) collective-permute-start(bf16[4,144,640]{2,1,0:T(8,128)(2,1)} %all-to-all-done.1.refs_0_), channel_id=1, source_target_pairs={{0,8},{8,0},{16,24},{24,16},{1,9},{9,1},{17,25},{25,17},{2,10},{10... | collective-permute-start | bytes 2211848 | tf_op jit(solution)/shard_map/ppermute | solution.py:382
  119.0 24.3 %collective-permute-start.18 = (bf16[4,144,640]{2,1,0:T(8,128)(2,1)}, bf16[4,144,640]{2,1,0:T(8,128)(2,1)S(1)}, u32[]{:S(2)}, u32[]{:S(2)}) collective-permute-start(bf16[4,144,640]{2,1,0:T(8,128)(2,1)} %collective-permute-done.16.refs_1_), channel_id=1, source_target_pairs={{0,8},{8,0},{16,24},{24,16},{1,9},{9,1},{17,25},{25,17},{2,10},{10... | collective-permute-start | bytes 2211848 | tf_op jit(solution)/shard_map/ppermute | solution.py:382
  123.9 6.4 %collective-permute-start.5 = (bf16[1,144,640]{2,1,0:T(8,128)(2,1)}, bf16[1,144,640]{2,1,0:T(8,128)(2,1)}, u32[]{:S(2)}, u32[]{:S(2)}) collective-permute-start(bf16[1,144,640]{2,1,0:T(8,128)(2,1)} %copy-done.11), channel_id=1, source_target_pairs={{0,16},{8,24},{16,0},{24,8},{1,17},{9,25},{17,1},{25,9},{2,18},{10... | collective-permute-start | bytes 552968 | tf_op jit(solution)/shard_map/ppermute | solution.py:380
  125.5 17.9 %copy-start.15 = (bf16[1,144,640]{2,1,0:T(8,128)(2,1)}, bf16[1,144,640]{2,1,0:T(8,128)(2,1)S(1)}, u32[]{:S(2)}) copy-start(bf16[1,144,640]{2,1,0:T(8,128)(2,1)S(1)} %collective-permute-done.6.refs_6_) | copy-start | bytes 552964
  125.5 6.4 %collective-permute-start.10 = (bf16[1,144,640]{2,1,0:T(8,128)(2,1)}, bf16[1,144,640]{2,1,0:T(8,128)(2,1)S(1)}, u32[]{:S(2)}, u32[]{:S(2)}) collective-permute-start(bf16[1,144,640]{2,1,0:T(8,128)(2,1)} %collective-permute-done.8.refs_8_), channel_id=1, source_target_pairs={{0,8},{8,0},{16,24},{24,16},{1,9},{9,1},{17,25},{25,17},{2,10},{10... | collective-permute-start | bytes 552968 | tf_op jit(solution)/shard_map/ppermute | solution.py:382
  130.4 5.9 %collective-permute-start.9 = (bf16[1,144,640]{2,1,0:T(8,128)(2,1)}, bf16[1,144,640]{2,1,0:T(8,128)(2,1)}, u32[]{:S(2)}, u32[]{:S(2)}) collective-permute-start(bf16[1,144,640]{2,1,0:T(8,128)(2,1)} %collective-permute-done.8.refs_8_), channel_id=1, source_target_pairs={{0,16},{8,24},{16,0},{24,8},{1,17},{9,25},{17,1},{25,9},{2,18},{10... | collective-permute-start | bytes 552968 | tf_op jit(solution)/shard_map/ppermute | solution.py:380
  131.9 12.0 %copy-start.16 = (bf16[1,144,640]{2,1,0:T(8,128)(2,1)}, bf16[1,144,640]{2,1,0:T(8,128)(2,1)S(1)}, u32[]{:S(2)}) copy-start(bf16[1,144,640]{2,1,0:T(8,128)(2,1)S(1)} %collective-permute-done.10.refs_10_) | copy-start | bytes 552964
  131.9 5.9 %collective-permute-start.14 = (bf16[1,144,640]{2,1,0:T(8,128)(2,1)}, bf16[1,144,640]{2,1,0:T(8,128)(2,1)S(1)}, u32[]{:S(2)}, u32[]{:S(2)}) collective-permute-start(bf16[1,144,640]{2,1,0:T(8,128)(2,1)} %collective-permute-done.12.refs_12_), channel_id=1, source_target_pairs={{0,8},{8,0},{16,24},{24,16},{1,9},{9,1},{17,25},{25,17},{2,10},{10... | collective-permute-start | bytes 552968 | tf_op jit(solution)/shard_map/ppermute | solution.py:382
  136.2 5.9 %collective-permute-start.13 = (bf16[1,144,640]{2,1,0:T(8,128)(2,1)}, bf16[1,144,640]{2,1,0:T(8,128)(2,1)}, u32[]{:S(2)}, u32[]{:S(2)}) collective-permute-start(bf16[1,144,640]{2,1,0:T(8,128)(2,1)} %collective-permute-done.12.refs_12_), channel_id=1, source_target_pairs={{0,16},{8,24},{16,0},{24,8},{1,17},{9,25},{17,1},{25,9},{2,18},{10... | collective-permute-start | bytes 552968 | tf_op jit(solution)/shard_map/ppermute | solution.py:380
  137.7 6.2 %copy-start.17 = (bf16[1,144,640]{2,1,0:T(8,128)(2,1)}, bf16[1,144,640]{2,1,0:T(8,128)(2,1)S(1)}, u32[]{:S(2)}) copy-start(bf16[1,144,640]{2,1,0:T(8,128)(2,1)S(1)} %collective-permute-done.14.refs_14_) | copy-start | bytes 552964
  137.7 4.3 %collective-permute-start.35 = (bf16[1,144,640]{2,1,0:T(8,128)(2,1)S(1)}, bf16[1,144,640]{2,1,0:T(8,128)(2,1)S(1)}, u32[]{:S(2)}, u32[]{:S(2)}) collective-permute-start(bf16[1,144,640]{2,1,0:T(8,128)(2,1)S(1)} %collective-permute-done.33.refs_3_), channel_id=1, source_target_pairs={{0,8},{8,0},{16,24},{24,16},{1,9},{9,1},{17,25},{25,17},{2,10},{10... | collective-permute-start | bytes 552968 | tf_op jit(solution)/shard_map/ppermute | solution.py:382
  142.1 11.9 %collective-permute-start.3 = (bf16[1,144,640]{2,1,0:T(8,128)(2,1)}, bf16[1,144,640]{2,1,0:T(8,128)(2,1)}, u32[]{:S(2)}, u32[]{:S(2)}) collective-permute-start(bf16[1,144,640]{2,1,0:T(8,128)(2,1)} %collective-permute-done.1.refs_1_), channel_id=1, source_target_pairs={{0,8},{8,0},{16,24},{24,16},{1,9},{9,1},{17,25},{25,17},{2,10},{10... | collective-permute-start | bytes 552968 | tf_op jit(solution)/shard_map/ppermute | solution.py:382
  142.7 11.7 %collective-permute-start.7 = (bf16[1,144,640]{2,1,0:T(8,128)(2,1)}, bf16[1,144,640]{2,1,0:T(8,128)(2,1)}, u32[]{:S(2)}, u32[]{:S(2)}) collective-permute-start(bf16[1,144,640]{2,1,0:T(8,128)(2,1)} %collective-permute-done.5.refs_5_), channel_id=1, source_target_pairs={{0,8},{8,0},{16,24},{24,16},{1,9},{9,1},{17,25},{25,17},{2,10},{10... | collective-permute-start | bytes 552968 | tf_op jit(solution)/shard_map/ppermute | solution.py:382
  143.3 0.9 copy-start.23
  143.3 11.3 %collective-permute-start.11 = (bf16[1,144,640]{2,1,0:T(8,128)(2,1)}, bf16[1,144,640]{2,1,0:T(8,128)(2,1)}, u32[]{:S(2)}, u32[]{:S(2)}) collective-permute-start(bf16[1,144,640]{2,1,0:T(8,128)(2,1)} %collective-permute-done.9.refs_9_), channel_id=1, source_target_pairs={{0,8},{8,0},{16,24},{24,16},{1,9},{9,1},{17,25},{25,17},{2,10},{10... | collective-permute-start | bytes 552968 | tf_op jit(solution)/shard_map/ppermute | solution.py:382
  143.4 1.0 copy-start.24
  143.4 11.6 %collective-permute-start.15 = (bf16[1,144,640]{2,1,0:T(8,128)(2,1)}, bf16[1,144,640]{2,1,0:T(8,128)(2,1)}, u32[]{:S(2)}, u32[]{:S(2)}) collective-permute-start(bf16[1,144,640]{2,1,0:T(8,128)(2,1)} %collective-permute-done.13.refs_13_), channel_id=1, source_target_pairs={{0,8},{8,0},{16,24},{24,16},{1,9},{9,1},{17,25},{25,17},{2,10},{10... | collective-permute-start | bytes 552968 | tf_op jit(solution)/shard_map/ppermute | solution.py:382
  154.0 14.3 %collective-permute-start.25 = (bf16[1,144,640]{2,1,0:T(8,128)(2,1)}, bf16[1,144,640]{2,1,0:T(8,128)(2,1)S(1)}, u32[]{:S(2)}, u32[]{:S(2)}) collective-permute-start(bf16[1,144,640]{2,1,0:T(8,128)(2,1)} %copy-done.7), channel_id=1, source_target_pairs={{0,8},{8,0},{16,24},{24,16},{1,9},{9,1},{17,25},{25,17},{2,10},{10... | collective-permute-start | bytes 552968 | tf_op jit(solution)/shard_map/ppermute | solution.py:382
  154.5 13.9 %collective-permute-start.29 = (bf16[1,144,640]{2,1,0:T(8,128)(2,1)}, bf16[1,144,640]{2,1,0:T(8,128)(2,1)S(1)}, u32[]{:S(2)}, u32[]{:S(2)}) collective-permute-start(bf16[1,144,640]{2,1,0:T(8,128)(2,1)} %copy-done.8), channel_id=1, source_target_pairs={{0,8},{8,0},{16,24},{24,16},{1,9},{9,1},{17,25},{25,17},{2,10},{10... | collective-permute-start | bytes 552968 | tf_op jit(solution)/shard_map/ppermute | solution.py:382
  154.6 13.7 %collective-permute-start.22 = (bf16[1,144,640]{2,1,0:T(8,128)(2,1)}, bf16[1,144,640]{2,1,0:T(8,128)(2,1)S(1)}, u32[]{:S(2)}, u32[]{:S(2)}) collective-permute-start(bf16[1,144,640]{2,1,0:T(8,128)(2,1)} %copy-done.10), channel_id=1, source_target_pairs={{0,8},{8,0},{16,24},{24,16},{1,9},{9,1},{17,25},{25,17},{2,10},{10... | collective-permute-start | bytes 552968 | tf_op jit(solution)/shard_map/ppermute | solution.py:382
  155.0 13.4 %collective-permute-start.26 = (bf16[1,144,640]{2,1,0:T(8,128)(2,1)}, bf16[1,144,640]{2,1,0:T(8,128)(2,1)}, u32[]{:S(2)}, u32[]{:S(2)}) collective-permute-start(bf16[1,144,640]{2,1,0:T(8,128)(2,1)} %copy-done.12), channel_id=1, source_target_pairs={{0,8},{8,0},{16,24},{24,16},{1,9},{9,1},{17,25},{25,17},{2,10},{10... | collective-permute-start | bytes 552968 | tf_op jit(solution)/shard_map/ppermute | solution.py:382
  155.1 10.1 %copy-start.1 = (bf16[4,288,640]{2,1,0:T(8,128)(2,1)}, bf16[4,288,640]{2,1,0:T(8,128)(2,1)S(1)}, u32[]{:S(2)}) copy-start(bf16[4,288,640]{2,1,0:T(8,128)(2,1)S(1)} %collective-permute-done.31.refs_1_) | copy-start | bytes 4423684
  155.1 13.2 %collective-permute-start.30 = (bf16[1,144,640]{2,1,0:T(8,128)(2,1)}, bf16[1,144,640]{2,1,0:T(8,128)(2,1)S(1)}, u32[]{:S(2)}, u32[]{:S(2)}) collective-permute-start(bf16[1,144,640]{2,1,0:T(8,128)(2,1)} %copy-done.13), channel_id=1, source_target_pairs={{0,8},{8,0},{16,24},{24,16},{1,9},{9,1},{17,25},{25,17},{2,10},{10... | collective-permute-start | bytes 552968 | tf_op jit(solution)/shard_map/ppermute | solution.py:382
  168.3 0.7 copy-start.19
  168.4 0.8 copy-start.20
  (6 other events, 4.0 us)
